TPU v7x, 128 devices: a whole 4x4x4 slice. The times are simulated.
128 devices in a mesh: fsdp: 2 (over core), ep: 64 (over z, y, x).
Axes of the slice: x: 4, y: 4, z: 4, core: 2. Of those that a mesh axis runs over, the one named last changes fastest.
Arguments:
- layer_in: bfloat16 [65536, 896], P(('fsdp', 'ep'))
- out_grad: bfloat16 [65536, 896], P(('fsdp', 'ep'))
- expert_ids: int32 [65536, 8], P(('fsdp', 'ep'))
- gate_vals: float32 [65536, 8], P(('fsdp', 'ep'))
- w_one: bfloat16 [64, 896, 640], P('ep', 'fsdp')
- w_two: bfloat16 [64, 640, 896], P('ep', None, 'fsdp')
- w_three: bfloat16 [64, 896, 640], P('ep', 'fsdp')
Outputs:
- output 1: bfloat16 [65536, 896], P(('fsdp', 'ep'))
- output 2: float32 [65536, 8], P(('fsdp', 'ep'))
- output 3: float32 [64, 896, 640], P('ep', 'fsdp')
- output 4: float32 [64, 640, 896], P('ep', None, 'fsdp')
- output 5: float32 [64, 896, 640], P('ep', 'fsdp')
All inputs are finite; a program needn't handle non-finite values.
Results may differ from a plain program's by a relative error of at most 0.0103469.
Values are sent between devices in bfloat16 or wider.
A program may use at most 1 GiB of HBM per device.

v0:
```python
import jax
import jax.numpy as jnp
from jax import lax
from jax.sharding import PartitionSpec as P


def capacity_of(tok_dev, top_k, experts):
    return max(8, ((tok_dev * top_k * 5) // (4 * experts) + 7) // 8 * 8)


def route_slots(expert_ids, experts, capacity):
    flat_ids = expert_ids.reshape(-1)
    onehot = (flat_ids[:, None] == jnp.arange(experts, dtype=jnp.int32)[None, :]).astype(jnp.int32)
    before = jnp.cumsum(onehot, axis=0) - onehot
    position = jnp.sum(before * onehot, axis=1)
    return jnp.where(position < capacity, flat_ids * capacity + position, experts * capacity)


def slot_sources(slot_of, gate_vals, tok_dev, places):
    top_k = gate_vals.shape[-1]
    token_of = jnp.arange(slot_of.shape[0], dtype=jnp.int32) // top_k
    source = jnp.full((places,), tok_dev, jnp.int32).at[slot_of].set(token_of, mode="drop")
    slot_gate = jnp.zeros((places,), jnp.float32).at[slot_of].set(gate_vals.reshape(-1), mode="drop")
    return source, slot_gate


def take_rows(rows, row_index):
    return jnp.take(rows, row_index, axis=0, mode="fill", fill_value=0)


def expert_grads(x_rows, dy_rows, gate_rows, w_one, w_two, w_three):
    h_one = jnp.einsum("pecd,edf->pecf", x_rows, w_one, preferred_element_type=jnp.float32)
    h_three = jnp.einsum("pecd,edf->pecf", x_rows, w_three, preferred_element_type=jnp.float32)
    sig_one = jax.nn.sigmoid(h_one)
    silu_one = h_one * sig_one
    act_bf = (silu_one * h_three).astype(jnp.bfloat16)
    y_rows = jnp.einsum("pecf,efd->pecd", act_bf, w_two, preferred_element_type=jnp.float32)
    gate_grad = jnp.sum(dy_rows.astype(jnp.float32) * y_rows, axis=-1)
    g_rows = (gate_rows[..., None] * dy_rows.astype(jnp.float32)).astype(jnp.bfloat16)
    d_act = jnp.einsum("pecd,efd->pecf", g_rows, w_two, preferred_element_type=jnp.float32)
    dh_one = (d_act * h_three * sig_one * (1.0 + h_one * (1.0 - sig_one))).astype(jnp.bfloat16)
    dh_three = (d_act * silu_one).astype(jnp.bfloat16)
    dx_rows = (jnp.einsum("pecf,edf->pecd", dh_one, w_one, preferred_element_type=jnp.float32) + jnp.einsum("pecf,edf->pecd", dh_three, w_three, preferred_element_type=jnp.float32)).astype(jnp.bfloat16)
    grad_one = jnp.einsum("pecd,pecf->edf", x_rows, dh_one, preferred_element_type=jnp.float32)
    grad_three = jnp.einsum("pecd,pecf->edf", x_rows, dh_three, preferred_element_type=jnp.float32)
    grad_two = jnp.einsum("pecf,pecd->efd", act_bf, g_rows, preferred_element_type=jnp.float32)
    return dx_rows, gate_grad, grad_one, grad_two, grad_three


def solution(mesh):
    ep_size = mesh.shape["ep"]
    tok_spec = P(("fsdp", "ep"), None)
    up_spec = P("ep", "fsdp", None)
    down_spec = P("ep", None, "fsdp")

    def per_device(layer_in, out_grad, expert_ids, gate_vals, w_one, w_two, w_three):
        tok_dev, hidden = layer_in.shape
        top_k = expert_ids.shape[1]
        local_experts = w_one.shape[0]
        experts = local_experts * ep_size
        capacity = capacity_of(tok_dev, top_k, experts)
        places = experts * capacity
        slot_of = route_slots(expert_ids, experts, capacity)
        source, slot_gate = slot_sources(slot_of, gate_vals, tok_dev, places)
        send_shape = (ep_size, local_experts, capacity, hidden)
        x_send = take_rows(layer_in, source).reshape(send_shape)
        dy_send = take_rows(out_grad, source).reshape(send_shape)
        gate_send = slot_gate.reshape(ep_size, local_experts, capacity)
        x_rows = lax.all_to_all(x_send, "ep", 0, 0, tiled=True)
        dy_rows = lax.all_to_all(dy_send, "ep", 0, 0, tiled=True)
        gate_rows = lax.all_to_all(gate_send, "ep", 0, 0, tiled=True)
        w_one_full = lax.all_gather(w_one, "fsdp", axis=1, tiled=True)
        w_three_full = lax.all_gather(w_three, "fsdp", axis=1, tiled=True)
        w_two_full = lax.all_gather(w_two, "fsdp", axis=2, tiled=True)
        dx_rows, gate_grad, grad_one, grad_two, grad_three = expert_grads(x_rows, dy_rows, gate_rows, w_one_full, w_two_full, w_three_full)
        dx_back = lax.all_to_all(dx_rows, "ep", 0, 0, tiled=True).reshape(places, hidden)
        gate_back = lax.all_to_all(gate_grad, "ep", 0, 0, tiled=True).reshape(places)
        dx_pick = take_rows(dx_back, slot_of).reshape(tok_dev, top_k, hidden)
        in_grad = jnp.sum(dx_pick, axis=1, dtype=jnp.float32).astype(jnp.bfloat16)
        gate_out = take_rows(gate_back, slot_of).reshape(tok_dev, top_k)
        grad_one = lax.psum_scatter(grad_one, "fsdp", scatter_dimension=1, tiled=True)
        grad_three = lax.psum_scatter(grad_three, "fsdp", scatter_dimension=1, tiled=True)
        grad_two = lax.psum_scatter(grad_two, "fsdp", scatter_dimension=2, tiled=True)
        return in_grad, gate_out, grad_one, grad_two, grad_three

    return jax.shard_map(per_device, mesh=mesh, in_specs=(tok_spec, tok_spec, tok_spec, tok_spec, up_spec, down_spec, up_spec), out_specs=(tok_spec, tok_spec, up_spec, down_spec, up_spec), check_vma=False)
```

profile of v0, /device:TPU:0, one launch (start us, length us, event | category | flops | bytes accessed | tf_op | source)
XLA Modules:
  0.0 698.8 jit_solution(7275006733707847668)
XLA Ops:
  7.2 0.9 copy.24
  8.1 0.1 eq.29
  8.3 0.1 eq.25
  8.5 0.4 copy-done.3
  8.8 0.1 fusion.51
  9.0 18.4 %reduce-window.6 = s32[64,32,128]{2,1,0:T(8,128)S(1)} reduce-window(s32[64,32,128]{2,1,0:T(8,128)S(1)} %fusion.51, s32[]{:T(128)} %constant.45.clone.1), window={size=1x1x128 pad=0_0x0_0x127_0}, to_apply=%region_0.0 | reduce-window | flops 33292288 | bytes 2097156 | tf_op jit(solution)/shard_map/reduce-window
  27.4 0.3 slice.16
  27.7 0.4 copy.38
  28.2 0.2 reduce-window.9
  28.4 0.3 broadcast_add_fusion
  28.7 0.2 mul.56
  28.9 0.1 copy.29
  29.0 0.2 reshape.202
  29.2 0.9 fusion.50
  30.1 0.6 copy-done.5
  30.7 15.5 %scatter_custom_fusion = f32[5120]{0:T(1024)S(1)} fusion(s32[4096]{0:T(1024)S(1)} %bitcast.184, f32[4096]{0:T(1024)S(1)} %reshape.202, f32[]{:T(128)} %constant.65.clone.1), kind=kCustom, calls=%fused_computation.82 | custom fusion | bytes 20484 | tf_op jit(solution)/shard_map/scatter | solution.py:23
  46.3 0.7 reshape.153
  47.0 11.6 %all-to-all-start = ((f32[64,1,80]{2,1,0:T(1,128)}), f32[64,1,80]{2,1,0:T(1,128)S(1)}, u32[]{:S(2)}, u32[]{:S(2)}) async-start(f32[64,1,80]{2,1,0:T(1,128)} %reshape.153), calls=%async_computation | async-start | bytes 65536 | tf_op jit(solution)/shard_map/all_to_all | solution.py:71
  58.6 15.5 %scatter_custom_fusion.1 = s32[5120]{0:T(1024)S(1)} fusion(s32[4096]{0:T(1024)S(1)} %bitcast.185, s32[4096]{0:T(1024)S(1)} %add_select_fusion, s32[]{:T(128)} %constant.66.clone.1), kind=kCustom, calls=%fused_computation.80 | custom fusion | bytes 20484 | tf_op jit(solution)/shard_map/scatter | solution.py:22
  74.2 22.3 %gather_fusion.2 = bf16[5120,896]{1,0:T(8,128)(2,1)} fusion(bf16[512,896]{1,0:T(8,128)(2,1)S(1)} %copy-done, s32[5120]{0:T(1024)S(1)} %fusion.52), kind=kCustom, calls=%fused_computation.clone | custom fusion | bytes 18370560 | tf_op jit(solution)/shard_map/jit(_take)/gather | solution.py:28
  96.5 22.3 %gather_fusion.3 = bf16[5120,896]{1,0:T(8,128)(2,1)} fusion(bf16[512,896]{1,0:T(8,128)(2,1)S(1)} %copy-done.2, s32[5120]{0:T(1024)S(1)} %fusion.52), kind=kCustom, calls=%fused_computation.1.clone | custom fusion | bytes 18370560 | tf_op jit(solution)/shard_map/jit(_take)/gather | solution.py:28
  118.8 14.9 %broadcast_select_fusion.1 = (bf16[5120,896]{1,0:T(8,128)(2,1)}, bf16[5120,896]{1,0:T(8,128)(2,1)}) fusion(bf16[5120,896]{1,0:T(8,128)(2,1)} %gather_fusion.2, pred[5120]{0:T(1024)(128)(4,1)S(1)} %compare_and_fusion.1, bf16[5120,896]{1,0:T(8,128)(2,1)} %gather_fusion.3), kind=kLoop, calls=%fused_computation.37 | loop fusion | flops 9175040 | bytes 36705280 | tf_op jit(solution)/shard_map/jit(_take)/select_n | solution.py:28
  133.7 128.3 %all_to_all.25 = bf16[64,1,80,896]{3,2,1,0:T(8,128)(2,1)} all-to-all(bf16[64,1,80,896]{3,2,1,0:T(8,128)(2,1)} %bitcast.179), channel_id=1, replica_groups=mesh['fsdp'=2,'ep'=64] {'ep'}, dimensions={0} | all-to-all | bytes 18350080 | tf_op jit(solution)/shard_map/all_to_all | solution.py:70
  262.0 13.1 %all-to-all-start.2 = ((bf16[64,1,80,896]{3,2,1,0:T(8,128)(2,1)}), bf16[64,1,80,896]{3,2,1,0:T(8,128)(2,1)}, u32[]{:S(2)}, u32[]{:S(2)}) async-start(bf16[64,1,80,896]{3,2,1,0:T(8,128)(2,1)} %bitcast.178), calls=%async_computation.2 | async-start | bytes 18350080 | tf_op jit(solution)/shard_map/all_to_all | solution.py:69
  275.1 0.0 all-gather.4.cloned.1.call-start
  275.1 0.7 all-gather.4.cloned.1.call-update
  275.8 0.0 all-gather.8.cloned.1.call-start
  275.9 0.7 all-gather.8.cloned.1.call-update
  276.6 0.0 all-gather.6.cloned.1.call-start
  276.6 0.7 all-gather.6.cloned.1.call-update
  277.3 0.5 all-reduce.3.cloned.1.call-start
  277.8 12.7 %all-gather.4.cloned.1.call-done = bf16[1,640,896]{1,2,0:T(8,128)(2,1)} async-done(((bf16[1,640,448]{1,2,0:T(8,128)(2,1)}), bf16[1,640,896]{1,2,0:T(8,128)(2,1)}) %all-gather.4.cloned.1.call-update) | async-done | bytes 1146896 | tf_op jit(solution)/shard_map/all_gather | solution.py:74
  290.5 13.7 %fusion.23 = f32[64,80,640]{2,1,0:T(8,128)} fusion(bf16[64,1,80,896]{3,2,1,0:T(8,128)(2,1)} %all_to_all.25, f32[64,80]{1,0:T(8,128)S(1)} %bitcast.187, bf16[1,640,896]{1,2,0:T(8,128)(2,1)} %all-gather.4.cloned.1.call-done), kind=kOutput, calls=%fused_computation.39 | convolution fusion | flops 5885788160 | bytes 23449600 | tf_op jit(solution)/shard_map/pecd,efd->pecf/dot_general | solution.py:40
  304.2 1.1 all-gather.8.cloned.1.call-done
  305.3 102.3 %all-to-all-done.2 = bf16[64,1,80,896]{3,2,1,0:T(8,128)(2,1)} async-done(((bf16[64,1,80,896]{3,2,1,0:T(8,128)(2,1)}), bf16[64,1,80,896]{3,2,1,0:T(8,128)(2,1)}, u32[]{:S(2)}, u32[]{:S(2)}) %all-to-all-start.2) | async-done | bytes 9175072 | tf_op jit(solution)/shard_map/all_to_all | solution.py:69
  407.7 13.6 %fusion.17 = f32[64,80,640]{2,1,0:T(8,128)} fusion(bf16[64,1,80,896]{3,2,1,0:T(8,128)(2,1)} %all-to-all-done.2, bf16[1,896,640]{2,1,0:T(8,128)(2,1)} %all-gather.8.cloned.1.call-done), kind=kOutput, calls=%fused_computation.32 | convolution fusion | flops 5872025600 | bytes 23429120 | tf_op jit(solution)/shard_map/pecd,edf->pecf/dot_general | solution.py:32
  421.3 22.6 %fusion.27 = (bf16[64,80,640]{2,1,0:T(8,128)(2,1)S(1)}, bf16[64,1,80,640]{3,2,0,1:T(8,128)(2,1)}, bf16[64,80,640]{2,1,0:T(8,128)(2,1)}) fusion(f32[64,80,640]{2,1,0:T(8,128)} %fusion.17, f32[64,80,640]{2,1,0:T(8,128)} %fusion.23, bf16[1,896,640]{2,1,0:T(8,128)(2,1)} %all-gather.6.cloned.1.call-done, bf16[64,1,80,896]{3,2,1,0:T(8,128)(2,1)} %all-to-all-done.2), kind=kOutput, calls=%fused_computation.43 | convolution fusion | flops 5921177600 | bytes 56197120 | tf_op jit(solution)/shard_map/pecd,edf->pecf/dot_general | solution.py:33
  443.9 2.7 copy-done.13
  446.6 10.6 %fusion.31 = f32[1,640,896]{2,1,0:T(8,128)S(1)} fusion(bf16[64,80,640]{2,1,0:T(8,128)(2,1)S(1)} %get-tuple-element.23, bf16[64,1,80,896]{3,2,1,0:T(8,128)(2,1)} %all_to_all.25, f32[64,80]{1,0:T(8,128)S(1)} %bitcast.188), kind=kOutput, calls=%fused_computation.47 | convolution fusion | flops 5885788160 | bytes 18042880 | tf_op jit(solution)/shard_map/pecf,pecd->efd/dot_general | solution.py:46
  457.2 3.7 copy.35
  461.0 0.0 all-reduce.3.cloned.1.call-update
  461.0 13.4 %fusion.1 = f32[64,80]{1,0:T(8,128)} fusion(bf16[64,1,80,896]{3,2,1,0:T(8,128)(2,1)} %all_to_all.25, bf16[64,80,640]{2,1,0:T(8,128)(2,1)} %copy-done.13, bf16[1,640,896]{1,2,0:T(8,128)(2,1)} %all-gather.4.cloned.1.call-done), kind=kOutput, calls=%fused_computation.9 | convolution fusion | flops 5885783040 | bytes 16896000 | tf_op jit(solution)/shard_map/pecf,efd->pecd/dot_general | solution.py:37
  474.4 15.1 %all-to-all-start.4 = ((f32[64,1,80]{2,1,0:T(1,128)}), f32[64,1,80]{2,1,0:T(1,128)S(1)}, u32[]{:S(2)}, u32[]{:S(2)}) async-start(f32[64,1,80]{2,1,0:T(1,128)} %bitcast.46), calls=%async_computation.4 | async-start | bytes 65536 | tf_op jit(solution)/shard_map/all_to_all | solution.py:77
  489.5 13.9 %fusion.29 = f32[64,80,896]{2,1,0:T(8,128)} fusion(bf16[64,1,80,640]{3,2,0,1:T(8,128)(2,1)} %get-tuple-element.24, bf16[1,896,640]{2,1,0:T(8,128)(2,1)S(1)} %copy-done.10), kind=kOutput, calls=%fused_computation.45 | convolution fusion | flops 5872025600 | bytes 26050560 | tf_op jit(solution)/shard_map/pecf,edf->pecd/dot_general | solution.py:43
  503.4 15.0 %fusion.11 = bf16[64,1,80,896]{3,2,1,0:T(8,128)(2,1)} fusion(f32[64,80,896]{2,1,0:T(8,128)} %fusion.29, bf16[64,80,640]{2,1,0:T(8,128)(2,1)} %get-tuple-element.25, bf16[1,896,640]{2,1,0:T(8,128)(2,1)S(1)} %copy-done.11), kind=kOutput, calls=%fused_computation.26 | convolution fusion | flops 5881200640 | bytes 35225600 | tf_op jit(solution)/shard_map/pecf,edf->pecd/dot_general | solution.py:43
  518.4 10.6 %all-to-all-start.3 = ((bf16[64,1,80,896]{3,2,1,0:T(8,128)(2,1)}), bf16[64,1,80,896]{3,2,1,0:T(8,128)(2,1)}, u32[]{:S(2)}, u32[]{:S(2)}) async-start(bf16[64,1,80,896]{3,2,1,0:T(8,128)(2,1)} %fusion.11), calls=%async_computation.3 | async-start | bytes 18350080 | tf_op jit(solution)/shard_map/all_to_all | solution.py:76
  529.0 0.0 reduce-scatter.5.cloned.1.call-start
  529.1 12.4 %fusion.39 = f32[1,896,640]{2,1,0:T(8,128)} fusion(bf16[64,80,640]{2,1,0:T(8,128)(2,1)} %get-tuple-element.25, bf16[64,1,80,896]{3,2,1,0:T(8,128)(2,1)} %all-to-all-done.2), kind=kOutput, calls=%fused_computation.49 | convolution fusion | flops 5872025600 | bytes 18022400 | tf_op jit(solution)/shard_map/pecd,pecf->edf/dot_general | solution.py:45
  541.5 0.0 reduce-scatter.3.cloned.1.call-start
  541.6 12.4 %fusion.34 = f32[1,896,640]{2,1,0:T(8,128)} fusion(bf16[64,1,80,640]{3,2,0,1:T(8,128)(2,1)} %get-tuple-element.24, bf16[64,1,80,896]{3,2,1,0:T(8,128)(2,1)} %all-to-all-done.2), kind=kOutput, calls=%fused_computation.48 | convolution fusion | flops 5872025600 | bytes 18022400 | tf_op jit(solution)/shard_map/pecd,pecf->edf/dot_general | solution.py:44
  554.0 0.2 reduce_sum.37
  554.2 0.6 dynamic-slice
  555.4 0.5 broadcast.139
  555.9 0.7 reduce.5
  556.7 0.1 reshape.165
  556.8 23.0 %gather_fusion.1 = f32[4096]{0:T(1024)S(1)} fusion(f32[5120]{0:T(1024)S(1)} %reshape.165, s32[4096]{0:T(1024)S(1)} %broadcast_clamp_fusion), kind=kCustom, calls=%fused_computation.3 | custom fusion | bytes 49152 | tf_op jit(solution)/shard_map/jit(_take)/gather | solution.py:28
  579.8 0.2 gather.18
  580.0 0.1 broadcast_select_fusion.2
  580.1 0.7 copy.36
  580.8 2.0 constant_dynamic-slice_fusion
  582.9 1.1 copy.37
  583.9 75.0 %all-to-all-done.3 = bf16[64,1,80,896]{3,2,1,0:T(8,128)(2,1)} async-done(((bf16[64,1,80,896]{3,2,1,0:T(8,128)(2,1)}), bf16[64,1,80,896]{3,2,1,0:T(8,128)(2,1)}, u32[]{:S(2)}, u32[]{:S(2)}) %all-to-all-start.3) | async-done | bytes 9175072 | tf_op jit(solution)/shard_map/all_to_all | solution.py:76
  659.0 24.7 %gather_fusion = bf16[4096,896]{1,0:T(8,128)(2,1)} fusion(bf16[5120,896]{1,0:T(8,128)(2,1)} %bitcast.38, s32[4096]{0:T(1024)S(1)} %broadcast_clamp_fusion), kind=kCustom, calls=%fused_computation.2 | custom fusion | bytes 14696448 | tf_op jit(solution)/shard_map/jit(_take)/gather | solution.py:28
  683.7 7.8 %fusion.25 = bf16[512,896]{1,0:T(8,128)(2,1)} fusion(bf16[4096,896]{1,0:T(8,128)(2,1)} %gather_fusion, pred[512,8]{1,0:T(8,128)(4,1)S(1)} %get-tuple-element.22), kind=kLoop, calls=%fused_computation.41 | loop fusion | flops 6881280 | bytes 8261632 | tf_op jit(solution)/shard_map/reduce_sum | solution.py:79
  (39 shorter events, 0.2 us)
Async XLA Ops:
  7.2 67.0 %copy-start = (bf16[512,896]{1,0:T(8,128)(2,1)S(1)}, bf16[512,896]{1,0:T(8,128)(2,1)}, u32[]{:S(2)}) copy-start(bf16[512,896]{1,0:T(8,128)(2,1)} %param.10) | copy-start | bytes 2752516
  7.2 21.7 %copy-start.9 = (f32[512,8]{0,1:T(8,128)S(1)}, f32[512,8]{0,1:T(8,128)}, u32[]{:S(2)}) copy-start(f32[512,8]{0,1:T(8,128)} %param.12) | copy-start | bytes 49156
  8.1 0.7 copy-start.3
  30.1 0.6 copy-start.5
  30.7 43.4 %copy-start.7 = (s32[4096,1]{0,1:T(1,128)}, s32[4096,1]{0,1:T(1,128)S(1)}, u32[]{:S(2)}) copy-start(s32[4096,1]{0,1:T(1,128)S(1)} %compare_select_fusion.1) | copy-start | bytes 49156
  47.0 86.7 %all-to-all-start = ((f32[64,1,80]{2,1,0:T(1,128)}), f32[64,1,80]{2,1,0:T(1,128)S(1)}, u32[]{:S(2)}, u32[]{:S(2)}) async-start(f32[64,1,80]{2,1,0:T(1,128)} %reshape.153), calls=%async_computation | async-start | bytes 65536 | tf_op jit(solution)/shard_map/all_to_all | solution.py:71
  74.2 22.3 %copy-start.2 = (bf16[512,896]{1,0:T(8,128)(2,1)S(1)}, bf16[512,896]{1,0:T(8,128)(2,1)}, u32[]{:S(2)}) copy-start(bf16[512,896]{1,0:T(8,128)(2,1)} %param.9) | copy-start | bytes 2752516
  262.0 145.6 %all-to-all-start.2 = ((bf16[64,1,80,896]{3,2,1,0:T(8,128)(2,1)}), bf16[64,1,80,896]{3,2,1,0:T(8,128)(2,1)}, u32[]{:S(2)}, u32[]{:S(2)}) async-start(bf16[64,1,80,896]{3,2,1,0:T(8,128)(2,1)} %bitcast.178), calls=%async_computation.2 | async-start | bytes 18350080 | tf_op jit(solution)/shard_map/all_to_all | solution.py:69
  275.1 15.5 %all-gather.4.cloned.1.call-start = ((), (), s32[]{:S(2)}) async-start(), calls=%async_computation.7 | async-start | bytes 1720320 | tf_op jit(solution)/shard_map/all_gather | solution.py:74
  275.8 29.5 %all-gather.8.cloned.1.call-start = ((), (), s32[]{:S(2)}) async-start(), calls=%async_computation.9 | async-start | bytes 1720320 | tf_op jit(solution)/shard_map/all_gather | solution.py:72
  276.6 144.7 %all-gather.6.cloned.1.call-start = ((), (), s32[]{:S(2)}) async-start(), calls=%async_computation.8 | async-start | bytes 1720320 | tf_op jit(solution)/shard_map/all_gather | solution.py:73
  277.3 303.5 %all-reduce.3.cloned.1.call-start = ((), (), s32[]{:S(2)}) async-start(), calls=%async_computation.12 | async-start | bytes 4587520
  443.9 2.7 copy-start.13
  461.0 28.5 %copy-start.10 = (bf16[1,896,640]{2,1,0:T(8,128)(2,1)S(1)}, bf16[1,896,640]{2,1,0:T(8,128)(2,1)}, u32[]{:S(2)}) copy-start(bf16[1,896,640]{2,1,0:T(8,128)(2,1)} %all-gather.8.cloned.1.call-done) | copy-start | bytes 3440644
  474.4 44.1 %all-to-all-start.4 = ((f32[64,1,80]{2,1,0:T(1,128)}), f32[64,1,80]{2,1,0:T(1,128)S(1)}, u32[]{:S(2)}, u32[]{:S(2)}) async-start(f32[64,1,80]{2,1,0:T(1,128)} %bitcast.46), calls=%async_computation.4 | async-start | bytes 65536 | tf_op jit(solution)/shard_map/all_to_all | solution.py:77
  489.5 13.9 %copy-start.11 = (bf16[1,896,640]{2,1,0:T(8,128)(2,1)S(1)}, bf16[1,896,640]{2,1,0:T(8,128)(2,1)}, u32[]{:S(2)}) copy-start(bf16[1,896,640]{2,1,0:T(8,128)(2,1)} %all-gather.6.cloned.1.call-done) | copy-start | bytes 3440644
  518.4 140.5 %all-to-all-start.3 = ((bf16[64,1,80,896]{3,2,1,0:T(8,128)(2,1)}), bf16[64,1,80,896]{3,2,1,0:T(8,128)(2,1)}, u32[]{:S(2)}, u32[]{:S(2)}) async-start(bf16[64,1,80,896]{3,2,1,0:T(8,128)(2,1)} %fusion.11), calls=%async_computation.3 | async-start | bytes 18350080 | tf_op jit(solution)/shard_map/all_to_all | solution.py:76
  529.0 162.5 %reduce-scatter.5.cloned.1.call-start = ((), (), s32[]{:S(2)}) async-start(), calls=%async_computation.11 | async-start | bytes 3440640 | tf_op jit(solution)/shard_map/reduce_scatter | solution.py:82
  541.5 12.5 %copy-start.6 = (s32[4096]{0:T(1024)S(1)}, s32[4096]{0:T(1024)}, u32[]{:S(2)}) copy-start(s32[4096]{0:T(1024)} %copy-done.5) | copy-start | bytes 49156
  541.5 12.7 %copy-start.12 = (u32[128]{0:T(128)S(1)}, u32[128]{0:T(128)}, u32[]{:S(2)}) copy-start(u32[128]{0:T(128)} %constant.78) | copy-start | bytes 1540
  541.5 13.9 %copy-start.8 = (s32[4096,1]{0,1:T(1,128)S(1)}, s32[4096,1]{0,1:T(1,128)}, u32[]{:S(2)}) copy-start(s32[4096,1]{0,1:T(1,128)} %copy-done.7) | copy-start | bytes 49156
  541.5 150.0 %reduce-scatter.3.cloned.1.call-start = ((), (), s32[]{:S(2)}) async-start(), calls=%async_computation.10 | async-start | bytes 3440640 | tf_op jit(solution)/shard_map/reduce_scatter | solution.py:81
  554.0 26.0 %copy-start.4 = (s32[512,8]{1,0:T(8,128)S(1)}, s32[512,8]{1,0:T(8,128)}, u32[]{:S(2)}) copy-start(s32[512,8]{1,0:T(8,128)} %copy-done.3) | copy-start | bytes 49156
  659.0 32.5 %copy-start.1 = (bf16[512,896]{1,0:T(8,128)(2,1)S(1)}, bf16[512,896]{1,0:T(8,128)(2,1)}, u32[]{:S(2)}) copy-start(bf16[512,896]{1,0:T(8,128)(2,1)} %param.10) | copy-start | bytes 2752516
Sparse Core Ops, SparseCore 0:
  277.5 12.9 all-gather.3
  292.2 13.0 all-gather.7
  307.0 13.0 all-gather.5
  461.1 32.4 all-reduce.2
  541.6 13.2 reduce-scatter.4
  557.7 13.4 reduce-scatter.2
where the time goes:
time: 711 us; the launch traced here: 699 us
  waiting for transfers between devices  193 us (27%)
  local copies, waits for them, and re-layouts  139 us (20%)
  blocking collectives  128 us (18%)
  matrix products  128 us (18%)
  starting transfers between devices  51 us (7%)
  other arithmetic  43.6 us (6%)
  between operations  15.6 us (2%)
    all_to_all x1, blocking collectives, per_device(): dy_rows = lax.all_to_all(dy_send, 'ep', 0, 0, tiled=True)  128 us
    all_to_all x1, waiting for transfers between devices, per_device(): x_rows = lax.all_to_all(x_send, 'ep', 0, 0, tiled=True)  102 us
    gather x5, local copies, waits for them, and re-layouts, take_rows(): return jnp.take(rows, row_index, axis=0, mode='fill', fill_value=0)  92.5 us
    all_to_all x1, waiting for transfers between devices, per_device(): lax.all_to_all(dx_rows, 'ep', 0, 0, tiled=True).reshape(places, hidden)  75 us
    dot_general x1, matrix products, expert_grads(): jnp.einsum('pecd,edf->pecf', x_rows, w_three, preferred_element_type=jnp....  22.6 us
    another operation x3, other arithmetic  19 us
    scatter x1, local copies, waits for them, and re-layouts, slot_sources(): jnp.zeros((places,), jnp.float32).at[slot_of]  15.5 us
    scatter x1, local copies, waits for them, and re-layouts, slot_sources(): jnp.full((places,), tok_dev, jnp.int32).at[slot_of]  15.5 us
  transfers between devices with their start and end apart: 10, of which 4 were waited for; matrix products, arithmetic and copies ran while one was open for 33% of the time, Pallas kernels for 0%

commit v1 on v0

v1 whole, which is shorter than its diff:
```python
import functools

import jax
import jax.numpy as jnp
from jax import lax
from jax.experimental import pallas as pl
from jax.experimental.pallas import tpu as pltpu
from jax.sharding import PartitionSpec as P

MESH = pl.DeviceIdType.MESH
ROWS = 16
BF16 = jnp.bfloat16
F32 = jnp.float32


def capacity_of(tok_dev, top_k, experts):
    return max(8, ((tok_dev * top_k * 5) // (4 * experts) + 7) // 8 * 8)


def column_groups(width):
    tiles = width // 128
    base = tiles // 3
    sizes = (base, base, tiles - 2 * base)
    starts = (0, base, 2 * base)
    return tuple((128 * s, 128 * n) for s, n in zip(starts, sizes))


def wait_bytes(ref, sem):
    pltpu.make_async_copy(ref, ref, sem).wait()


def dot(a, b, dims=((1,), (0,))):
    return lax.dot_general(a, b, (dims, ((), ())), preferred_element_type=F32)


def moe_kernel(ring, cap, x_hbm, u_hbm, ids_ref, gates_ref, w1_hbm, w3_hbm, w2_hbm,
               dx_out, dg_out, g1_out, g3_out, g2_out, mid_hbm, fin_hbm, b1_hbm, b2_hbm, b3_hbm,
               xa, pos0, pos1, pos2, line0, line1, line2, sg0, sg1, sg2, sg3, dg0, dg1, dg2, dg3,
               gbuf, xv, dxb, bv, acc, w1, w3, w2, dw1, dw3, dw2, dw1r, dw3r, dw2r,
               ld_s, ag_s, ag_r, p_s, p_r, w_s, w_r, sg_s, sg_r, dg_s, dg_r,
               s2_s, s2_r, s2_l, s3_s, s3_r, r1_s, r1_r, r1_l, r2_s, r2_r, r3_s, r3_r,
               cl_s, bl_s, dw_s, dw_r, out_s):
    tok, hidden = x_hbm.shape
    top_k = ids_ref.shape[0]
    half = w2_hbm.shape[1]
    chunks = cap // ROWS
    plane = ring * ring
    block = plane * ROWS
    cols = [pl.ds(s, n) for s, n in column_groups(hidden)]
    pos = (pos0, pos1, pos2)
    line = (line0, line1, line2)
    strides = (ring * ring, ring, 1)
    me = lax.axis_index("ep")
    core = lax.axis_index("fsdp")
    other = {"fsdp": 1 - core}
    coord = [lax.rem(me // s, ring) for s in strides]
    rest = pl.ds(1, ring - 1)

    def peer(axis, d):
        c = coord[axis]
        return {"ep": me + (lax.rem(c + d, ring) - c) * strides[axis]}

    def at(ref, lead, sel, col):
        return ref.at[(*lead, *(sel.get(a, slice(None)) for a in range(3)), slice(None), col)]

    def send(src, dst, s_sem, r_sem, device):
        pltpu.make_async_remote_copy(src_ref=src, dst_ref=dst, send_sem=s_sem, recv_sem=r_sem,
                                     device_id=device, device_id_type=MESH).start()

    def expert_column(order):
        row = lax.broadcasted_iota(jnp.int32, (ring ** 3, 1), 0)
        digits = (row // (ring * ring), lax.rem(row // ring, ring), lax.rem(row, ring))
        total = jnp.zeros_like(row)
        for digit, axis in zip(digits, order):
            total = total + lax.rem(digit + coord[axis], ring) * strides[axis]
        return total

    own = [
        pltpu.make_async_copy(x_hbm, xa.at[0, 0], ld_s.at[0]),
        pltpu.make_async_copy(u_hbm, xa.at[1, 0], ld_s.at[1]),
        pltpu.make_async_copy(w1_hbm, w1.at[core], ld_s.at[2]),
        pltpu.make_async_copy(w3_hbm, w3.at[core], ld_s.at[3]),
        pltpu.make_async_copy(w2_hbm, w2.at[core], ld_s.at[4]),
    ]
    for copy in own:
        copy.start()

    barrier = pltpu.get_barrier_semaphore()
    for axis in range(3):
        for d in range(1, ring):
            pl.semaphore_signal(barrier, inc=1, device_id=peer(axis, d), device_id_type=MESH)
    pl.semaphore_signal(barrier, inc=1, device_id=other, device_id_type=MESH)
    pl.semaphore_wait(barrier, 3 * (ring - 1) + 1)

    def gather_line(array, ref):
        for d in range(1, ring):
            for p in range(3):
                send(ref.at[:, cols[p]], xa.at[array, ring - d, :, cols[p]],
                     ag_s.at[array, p], ag_r.at[array, p], peer(p, d))

    gather_line(0, x_hbm)
    for i, (src, dst) in enumerate(((w1_hbm, w1), (w3_hbm, w3), (w2_hbm, w2))):
        send(src, dst.at[core], w_s.at[i], w_r.at[i], other)

    earlier = (lax.broadcasted_iota(jnp.int32, (tok, tok), 0) < lax.broadcasted_iota(jnp.int32, (tok, tok), 1))
    earlier = jnp.where(earlier, 1.0, 0.0).astype(BF16)
    for p, order in enumerate(((0, 1, 2), (1, 0, 2), (2, 0, 1))):
        expert = expert_column(order)
        chosen = jnp.zeros((ring ** 3, tok), F32)
        for j in range(top_k):
            chosen = chosen + jnp.where(ids_ref[j:j + 1, :] == expert, 1.0, 0.0)
        before = dot(chosen.astype(BF16), earlier)
        place = jnp.where((chosen > 0.5) & (before < cap), before, -1.0)
        pos[p][...] = place.reshape(ring, plane, tok)
        for d in range(1, ring):
            send(pos[p].at[d], line[p].at[ring - d], p_s.at[p], p_r.at[p], peer(p, d))
    gather_line(1, u_hbm)

    expert = expert_column((0, 1, 2))
    place = pos0[...].reshape(ring ** 3, tok)
    gate = jnp.zeros((ring ** 3, tok), F32)
    for j in range(top_k):
        gate = gate + jnp.where(ids_ref[j:j + 1, :] == expert, gates_ref[j:j + 1, :], 0.0)
    lane = lax.broadcasted_iota(jnp.int32, (ring ** 3, 128), 1)

    def gate_place(r, table):
        picked = jnp.sum(jnp.where(place == r.astype(F32), gate, 0.0), axis=1, keepdims=True)
        return jnp.where(lane == r, picked, table)

    table = lax.fori_loop(0, cap, gate_place, jnp.zeros((ring ** 3, 128), F32))
    sg0[...] = table.reshape(ring, ring, ring, 1, 128)

    def small_start(axis, src, dst, s_sem, r_sem):
        sel = lambda i: tuple(i if a == axis else slice(None) for a in range(3))
        for d in range(1, ring):
            send(src.at[sel(d)], dst.at[sel(ring - d)], s_sem.at[axis], r_sem.at[axis], peer(axis, d))
        dst[sel(pl.ds(0, 1))] = src[sel(pl.ds(0, 1))]

    def small_wait(axis, dst, r_sem):
        wait_bytes(dst.at[tuple(rest if a == axis else slice(None) for a in range(3))], r_sem.at[axis])

    small_start(0, sg0, sg1, sg_s, sg_r)
    for ref in (dw1, dw3, dw2, acc, dg0):
        ref[...] = jnp.zeros_like(ref)
    for copy in own:
        copy.wait()
    for p in range(3):
        wait_bytes(line[p].at[rest], p_r.at[p])

    def one_hot(places, first):
        n = places.shape[0]
        row = lax.broadcasted_iota(jnp.int32, (n, ROWS, tok), 1) + first
        hit = places[:, None, :] == row.astype(F32)
        return jnp.where(hit, 1.0, 0.0).astype(BF16).reshape(n * ROWS, tok)

    def dispatch(c):
        slot = lax.rem(c, 2)
        for array in range(2):
            for p in range(3):
                axis = (p + 1) % 3

                @pl.when(c == 0)
                def _():
                    wait_bytes(xa.at[array, rest, :, cols[p]], ag_r.at[array, p])

                @pl.when(c >= 2)
                def _():
                    wait_bytes(at(gbuf, (array, slot), {axis: rest}, cols[p]), s2_s.at[array, slot, p])

                width = column_groups(hidden)[p][1]
                for d in range(ring):
                    places = pos[p][0] if d == 0 else line[p][d]
                    rows = dot(one_hot(places, c * ROWS), xa[array, d, :, cols[p]]).astype(BF16)
                    idx = tuple(d if a == p else slice(None) for a in range(3))
                    gbuf[(array, slot, *idx, slice(None), cols[p])] = rows.reshape(ring, ring, ROWS, width)
                for d in range(1, ring):
                    send(at(gbuf, (array, slot), {axis: d}, cols[p]),
                         at(mid_hbm, (array, c), {axis: ring - d}, cols[p]),
                         s2_s.at[array, slot, p], s2_r.at[array, c, p], peer(axis, d))
                pltpu.make_async_copy(at(gbuf, (array, slot), {axis: 0}, cols[p]),
                                      at(mid_hbm, (array, c), {axis: 0}, cols[p]), s2_l.at[array, c, p]).start()

    def forward(c):
        for array in range(2):
            for p in range(3):
                axis, last = (p + 1) % 3, (p + 2) % 3
                wait_bytes(at(mid_hbm, (array, c), {axis: rest}, cols[p]), s2_r.at[array, c, p])
                wait_bytes(at(mid_hbm, (array, c), {axis: 0}, cols[p]), s2_l.at[array, c, p])
                for d in range(1, ring):
                    send(at(mid_hbm, (array, c), {last: d}, cols[p]),
                         at(fin_hbm, (array, c), {last: ring - d}, cols[p]),
                         s3_s.at[array, c, p], s3_r.at[array, c, p], peer(last, d))

    def compute(c):
        slot = lax.rem(c, 2)
        for array in range(2):
            for p in range(3):
                last = (p + 2) % 3
                wait_bytes(at(fin_hbm, (array, c), {last: rest}, cols[p]), s3_r.at[array, c, p])
                for src, part in ((fin_hbm, rest), (mid_hbm, 0)):
                    pltpu.make_async_copy(at(src, (array, c), {last: part}, cols[p]),
                                          at(xv, (array,), {last: part}, cols[p]), cl_s.at[array, p]).start()

        @pl.when(c >= 2)
        def _():
            for p in range(3):
                wait_bytes(at(dxb, (slot,), {(p + 2) % 3: rest}, cols[p]), r1_s.at[slot, p])

        for array in range(2):
            for p in range(3):
                wait_bytes(at(xv, (array,), {}, cols[p]), cl_s.at[array, p])

        def step(m, carry):
            x = xv[0, m].reshape(block, hidden)
            u = xv[1, m].reshape(block, hidden)
            w1_full = w1[...].reshape(hidden, -1)
            w3_full = w3[...].reshape(hidden, -1)
            hit = (lax.broadcasted_iota(jnp.int32, (plane, ROWS, 128), 2)
                   == lax.broadcasted_iota(jnp.int32, (plane, ROWS, 128), 1) + c * ROWS)
            s = jnp.sum(jnp.where(hit, sg3[m].reshape(plane, 1, 128), 0.0), axis=2, keepdims=True).reshape(block, 1)
            h1 = dot(x, w1_full)
            h3 = dot(x, w3_full)
            sig = jax.nn.sigmoid(h1)
            silu = h1 * sig
            act = (silu * h3).astype(BF16)
            u32 = u.astype(F32)
            g = (s * u32).astype(BF16)
            da = jnp.zeros_like(h1)
            dg = jnp.zeros((block, 1), F32)
            for i in range(2):
                span = slice(i * half, (i + 1) * half)
                g_half = g[:, span]
                y = dot(act, w2[i])
                dg = dg + jnp.sum(u32[:, span] * y, axis=1, keepdims=True)
                da = da + dot(g_half, w2[i], ((1,), (1,)))
                dw2[i] += dot(act, g_half, ((0,), (0,)))
            dh1 = (da * h3 * sig * (1.0 + h1 * (1.0 - sig))).astype(BF16)
            dh3 = (da * silu).astype(BF16)
            dx = dot(dh1, w1_full, ((1,), (1,))) + dot(dh3, w3_full, ((1,), (1,)))
            dxb[slot, m] = dx.astype(BF16).reshape(ring, ring, ROWS, hidden)
            dw1[...] += dot(x, dh1, ((0,), (0,))).reshape(dw1.shape)
            dw3[...] += dot(x, dh3, ((0,), (0,))).reshape(dw3.shape)
            spread = jnp.sum(jnp.where(hit, dg.reshape(plane, ROWS, 1), 0.0), axis=1, keepdims=True)
            dg0[m] += spread.reshape(ring, ring, 1, 128)
            return carry

        lax.fori_loop(0, ring, step, 0)
        for p in range(3):
            last = (p + 2) % 3
            for d in range(1, ring):
                send(at(dxb, (slot,), {last: d}, cols[p]), at(b1_hbm, (c,), {last: ring - d}, cols[p]),
                     r1_s.at[slot, p], r1_r.at[c, p], peer(last, d))
            pltpu.make_async_copy(at(dxb, (slot,), {last: 0}, cols[p]), at(b1_hbm, (c,), {last: 0}, cols[p]),
                                  r1_l.at[c, p]).start()

    def back_two(c):
        for p in range(3):
            axis, last = (p + 1) % 3, (p + 2) % 3
            wait_bytes(at(b1_hbm, (c,), {last: rest}, cols[p]), r1_r.at[c, p])
            wait_bytes(at(b1_hbm, (c,), {last: 0}, cols[p]), r1_l.at[c, p])
            for d in range(1, ring):
                send(at(b1_hbm, (c,), {axis: d}, cols[p]), at(b2_hbm, (c,), {axis: ring - d}, cols[p]),
                     r2_s.at[c, p], r2_r.at[c, p], peer(axis, d))

    def back_three(c):
        for p in range(3):
            axis = (p + 1) % 3
            wait_bytes(at(b2_hbm, (c,), {axis: rest}, cols[p]), r2_r.at[c, p])
            for d in range(1, ring):
                for src, part in ((b2_hbm, rest), (b1_hbm, 0)):
                    send(at(src, (c,), {p: d, axis: part}, cols[p]),
                         at(b3_hbm, (c,), {p: ring - d, axis: part}, cols[p]),
                         r3_s.at[c, p], r3_r.at[c, p], peer(p, d))

    def combine(c):
        for p in range(3):
            axis = (p + 1) % 3
            wait_bytes(at(b3_hbm, (c,), {p: rest}, cols[p]), r3_r.at[c, p])
            for src, sel in ((b3_hbm, {p: rest}), (b2_hbm, {p: 0, axis: rest}), (b1_hbm, {p: 0, axis: 0})):
                pltpu.make_async_copy(at(src, (c,), sel, cols[p]), at(bv, (), sel, cols[p]), bl_s.at[p]).start()
        for p in range(3):
            wait_bytes(at(bv, (), {}, cols[p]), bl_s.at[p])

        def step(m, carry):
            acc[...] += dot(one_hot(pos0[m], c * ROWS), bv[m].reshape(block, hidden), ((0,), (0,)))
            return carry

        lax.fori_loop(0, ring, step, 0)

    grads = ((dw1, dw1r, g1_out), (dw3, dw3r, g3_out), (dw2, dw2r, g2_out))

    def gate_grads():
        small_wait(0, dg3, dg_r)
        expert = expert_column((0, 1, 2))
        place = pos0[...].reshape(ring ** 3, tok)
        values = dg3[...].reshape(ring ** 3, 128)

        def pick(r, total):
            value = jnp.sum(jnp.where(lane == r, values, 0.0), axis=1, keepdims=True)
            return total + jnp.where(place == r.astype(F32), value, 0.0)

        dense = lax.fori_loop(0, cap, pick, jnp.zeros((ring ** 3, tok), F32))
        for j in range(top_k):
            dg_out[j:j + 1, :] = jnp.sum(jnp.where(ids_ref[j:j + 1, :] == expert, dense, 0.0), axis=0, keepdims=True)

    def tick(k, carry):
        @pl.when(k < chunks)
        def _():
            dispatch(k)

        @pl.when(k == 0)
        def _():
            small_wait(0, sg1, sg_r)
            small_start(1, sg1, sg2, sg_s, sg_r)

        @pl.when(k == 1)
        def _():
            small_wait(1, sg2, sg_r)
            small_start(2, sg2, sg3, sg_s, sg_r)

        @pl.when((k >= 1) & (k <= chunks))
        def _():
            forward(k - 1)

        @pl.when((k >= 4) & (k < chunks + 4))
        def _():
            back_three(k - 4)

        @pl.when((k >= 3) & (k < chunks + 3))
        def _():
            back_two(k - 3)

        @pl.when(k == 2)
        def _():
            small_wait(2, sg3, sg_r)
            for i, ref in enumerate((w1, w3, w2)):
                wait_bytes(ref.at[1 - core], w_r.at[i])

        @pl.when((k >= 2) & (k < chunks + 2))
        def _():
            compute(k - 2)

        @pl.when(k == chunks + 1)
        def _():
            small_start(2, dg0, dg1, dg_s, dg_r)
            for i, (mine, theirs, _) in enumerate(grads):
                send(mine.at[1 - core], theirs, dw_s.at[i], dw_r.at[i], other)

        @pl.when(k == chunks + 2)
        def _():
            small_wait(2, dg1, dg_r)
            small_start(1, dg1, dg2, dg_s, dg_r)
            for i, (mine, theirs, out) in enumerate(grads):
                wait_bytes(theirs, dw_r.at[i])
                theirs[...] += mine[core]
                pltpu.make_async_copy(theirs, out, out_s.at[i]).start()

        @pl.when(k == chunks + 3)
        def _():
            small_wait(1, dg2, dg_r)
            small_start(0, dg2, dg3, dg_s, dg_r)

        @pl.when(k == chunks + 4)
        def _():
            gate_grads()

        @pl.when(k >= 5)
        def _():
            combine(k - 5)

        return carry

    lax.fori_loop(0, chunks + 5, tick, 0)
    dx_out[...] = acc[...].astype(BF16)

    for array in range(2):
        for p in range(3):
            wait_bytes(xa.at[array, rest, :, cols[p]], ag_s.at[array, p])
    for p in range(3):
        wait_bytes(line[p].at[rest], p_s.at[p])
        wait_bytes(sg1.at[rest], sg_s.at[p])
        wait_bytes(dg1.at[rest], dg_s.at[p])
    for i, ref in enumerate((w1, w3, w2)):
        wait_bytes(ref.at[1 - core], w_s.at[i])
    for i, (mine, theirs, out) in enumerate(grads):
        wait_bytes(theirs, dw_s.at[i])
        wait_bytes(out, out_s.at[i])
    for slot in range(2):
        for p in range(3):
            axis, last = (p + 1) % 3, (p + 2) % 3
            for array in range(2):
                wait_bytes(at(gbuf, (array, slot), {axis: rest}, cols[p]), s2_s.at[array, slot, p])
            wait_bytes(at(dxb, (slot,), {last: rest}, cols[p]), r1_s.at[slot, p])

    def drain(c, carry):
        for p in range(3):
            axis, last = (p + 1) % 3, (p + 2) % 3
            for array in range(2):
                wait_bytes(at(fin_hbm, (array, c), {last: rest}, cols[p]), s3_s.at[array, c, p])
            wait_bytes(at(b2_hbm, (c,), {axis: rest}, cols[p]), r2_s.at[c, p])
            wait_bytes(at(b3_hbm, (c,), {p: rest}, cols[p]), r3_s.at[c, p])
        return carry

    lax.fori_loop(0, chunks, drain, 0)


def build(mesh, capacity=None):
    ep_size = mesh.shape["ep"]
    ring = round(ep_size ** (1 / 3))
    tok_spec = P(("fsdp", "ep"), None)
    up_spec = P("ep", "fsdp", None)
    down_spec = P("ep", None, "fsdp")

    def per_device(layer_in, out_grad, expert_ids, gate_vals, w_one, w_two, w_three):
        tok, hidden = layer_in.shape
        top_k = expert_ids.shape[1]
        _, half, width = w_one.shape
        cap = capacity or capacity_of(tok, top_k, ep_size)
        chunks = cap // ROWS
        cube = (ring, ring, ring, ROWS, hidden)
        table = (ring, ring * ring, tok)
        small = (ring, ring, ring, 1, 128)
        vmem, dma = pltpu.VMEM, pltpu.SemaphoreType.DMA
        hbm = pl.BlockSpec(memory_space=pl.ANY)
        local = pl.BlockSpec(memory_space=pltpu.VMEM)
        sds = jax.ShapeDtypeStruct
        outs = pl.pallas_call(
            functools.partial(moe_kernel, ring, cap),
            out_shape=[
                sds((tok, hidden), BF16), sds((top_k, tok), F32),
                sds((half, width), F32), sds((half, width), F32), sds((width, half), F32),
                sds((2, chunks, *cube), BF16), sds((2, chunks, *cube), BF16),
                sds((chunks, *cube), BF16), sds((chunks, *cube), BF16), sds((chunks, *cube), BF16),
            ],
            in_specs=[hbm, hbm, local, local, hbm, hbm, hbm],
            out_specs=[local, local] + [hbm] * 8,
            scratch_shapes=[
                vmem((2, ring, tok, hidden), BF16),
                *[vmem(table, F32)] * 6,
                *[vmem(small, F32)] * 8,
                vmem((2, 2, *cube), BF16), vmem((2, *cube), BF16), vmem((2, *cube), BF16), vmem(cube, BF16),
                vmem((tok, hidden), F32),
                vmem((2, half, width), BF16), vmem((2, half, width), BF16), vmem((2, width, half), BF16),
                vmem((2, half, width), F32), vmem((2, half, width), F32), vmem((2, width, half), F32),
                vmem((half, width), F32), vmem((half, width), F32), vmem((width, half), F32),
                dma((5,)), dma((2, 3)), dma((2, 3)), dma((3,)), dma((3,)), dma((3,)), dma((3,)),
                dma((3,)), dma((3,)), dma((3,)), dma((3,)),
                dma((2, 2, 3)), dma((2, chunks, 3)), dma((2, chunks, 3)),
                dma((2, chunks, 3)), dma((2, chunks, 3)),
                dma((2, 3)), dma((chunks, 3)), dma((chunks, 3)),
                dma((chunks, 3)), dma((chunks, 3)), dma((chunks, 3)), dma((chunks, 3)),
                dma((2, 3)), dma((3,)), dma((3,)), dma((3,)), dma((3,)),
            ],
            compiler_params=pltpu.CompilerParams(
                collective_id=0, has_side_effects=True, vmem_limit_bytes=63 << 20
            ),
            name="moe_backward",
        )(layer_in, out_grad, expert_ids.T, gate_vals.T, w_one[0], w_three[0], w_two[0])
        dx, dg, g1, g3, g2 = outs[:5]
        return dx, dg.T, g1[None], g2[None], g3[None]

    return jax.shard_map(per_device, mesh=mesh,
                         in_specs=(tok_spec, tok_spec, tok_spec, tok_spec, up_spec, down_spec, up_spec),
                         out_specs=(tok_spec, tok_spec, up_spec, down_spec, up_spec), check_vma=False)


def solution(mesh):
    return build(mesh)
```

time: 711 us -> 311 us (0.44); the launches traced: 699 us -> 310 us
  Pallas kernels: 0 us -> 301 us
  waiting for transfers between devices: 193 us -> 0 us
  local copies, waits for them, and re-layouts: 139 us -> 8.54 us
  matrix products: 128 us -> 0 us
  blocking collectives: 128 us -> 0 us
  starting transfers between devices: 51 us -> 0 us
  other arithmetic: 43.6 us -> 0 us
  between operations: 15.6 us -> 0.65 us
    pallas_call x0 -> x1, Pallas kernels: none -> 301 us  [per_device(): pl.pallas_call(functools.partial(moe_kernel, ring, cap), out_shape=[sds((...]
    all_to_all x4 -> x0, waiting for transfers between devices: 177 us -> none  [the longest x1 102 us: per_device(): x_rows = lax.all_to_all(x_send, 'ep', 0, 0, tiled=True)]
    all_to_all x1 -> x0, blocking collectives: 128 us -> none  [per_device(): dy_rows = lax.all_to_all(dy_send, 'ep', 0, 0, tiled=True)]
    dot_general x9 -> x0, matrix products: 128 us -> none  [the longest x1 22.6 us: expert_grads(): jnp.einsum('pecd,edf->pecf', x_rows, w_three, preferred_element_type=jnp....]
    gather x5 -> x0, local copies, waits for them, and re-layouts: 92.5 us -> none  [take_rows(): return jnp.take(rows, row_index, axis=0, mode='fill', fill_value=0)]
    all_to_all x4 -> x0, starting transfers between devices: 50.3 us -> none  [the longest x1 15.1 us: per_device(): lax.all_to_all(gate_grad, 'ep', 0, 0, tiled=True).reshape(places)]
    scatter x2 -> x0, local copies, waits for them, and re-layouts: 31.1 us -> none  [the longest x1 15.5 us: slot_sources(): jnp.zeros((places,), jnp.float32).at[slot_of]]
    another operation x3 -> x0, other arithmetic: 19 us -> none
  transfers between devices with their start and end apart: 10 -> 0, of which waited for: 4 -> 0; matrix products, arithmetic and copies ran while one was open for 33% -> 0% of each run, Pallas kernels for 0% -> 0%
where the time goes in v1:
time: 311 us; the launch traced here: 310 us
  Pallas kernels  301 us (97%)
  local copies, waits for them, and re-layouts  8.54 us (3%)
    pallas_call x1, Pallas kernels, per_device(): pl.pallas_call(functools.partial(moe_kernel, ring, cap), out_shape=[sds((...  301 us
    unnamed x14, local copies, waits for them, and re-layouts  8.54 us

profile of v1, /device:TPU:0, one launch (start us, length us, event | category | flops | bytes accessed | tf_op | source)
XLA Modules:
  0.0 310.3 jit_solution(6711731080337699348)
XLA Ops:
  0.6 2.1 copy.12
  2.8 301.1 %moe_backward.1 = (bf16[512,896]{1,0:T(8,128)(2,1)}, f32[8,512]{1,0:T(8,128)}, f32[448,640]{1,0:T(8,128)}, f32[448,640]{1,0:T(8,128)}, f32[640,448]{1,0:T(8,128)...) custom-call(bf16[512,896]{1,0:T(8,128)(2,1)} %x_hbm.1, ...), custom_call_target="tpu_custom_call" | custom-call | tf_op jit(solution)/shard_map/moe_backward/pallas_call | solution.py:427
  303.9 0.0 copy-start.2
  303.9 2.8 copy.13
  306.7 0.0 copy-done.2
  306.7 0.0 copy-start.3
  306.7 0.0 copy-start.1
  306.7 0.9 copy.18
  307.6 0.0 copy-done.3
  307.6 0.0 copy-start
  307.6 0.6 copy.19
  308.2 0.1 copy-done.1
  308.3 1.0 copy.20
  309.3 0.0 copy-done
  309.3 1.0 copy.21
Async XLA Ops:
  303.9 2.8 copy-start.2
  306.7 0.9 copy-start.3
  306.7 1.6 copy-start.1
  307.6 1.7 copy-start

commit v2 on v1

v2 whole, which is shorter than its diff:
```python
import functools

import jax
import jax.numpy as jnp
from jax import lax
from jax.experimental import pallas as pl
from jax.experimental.pallas import tpu as pltpu
from jax.sharding import PartitionSpec as P

MESH = pl.DeviceIdType.MESH
ROWS = 16
BF16 = jnp.bfloat16
F32 = jnp.float32


def capacity_of(tok_dev, top_k, experts):
    return max(8, ((tok_dev * top_k * 5) // (4 * experts) + 7) // 8 * 8)


def column_groups(width, wide):
    tiles = width // 128
    base = tiles // 3
    sizes = [base + (tiles - 3 * base if p == wide else 0) for p in range(3)]
    starts = [sum(sizes[:p]) for p in range(3)]
    return [(128 * s, 128 * n) for s, n in zip(starts, sizes)]


def wait_bytes(ref, sem):
    pltpu.make_async_copy(ref, ref, sem).wait()


def dot(a, b, dims=((1,), (0,))):
    return lax.dot_general(a, b, (dims, ((), ())), preferred_element_type=F32)


def at(ref, lead, sel, col):
    return ref.at[(*lead, *(sel.get(a, slice(None)) for a in range(3)), slice(None), col)]


def one_hot(places, first):
    n, tok = places.shape
    row = lax.broadcasted_iota(jnp.int32, (n, ROWS, tok), 1) + first
    hit = places[:, None, :] == row.astype(F32)
    return jnp.where(hit, 1.0, 0.0).astype(BF16).reshape(n * ROWS, tok)


def returned_parts(ring, p):
    axis, rest = (p + 1) % 3, pl.ds(1, ring - 1)
    return ({p: 0, axis: 0}, {p: 0, axis: rest}, {p: rest})


def moe_kernel(ring, cap, x_hbm, u_hbm, ids_ref, gates_ref, w1_hbm, w3_hbm, w2_hbm,
               dg_out, acc_out, pos_out, g1_out, g3_out, g2_out, mid_hbm, fin_hbm, b1_hbm, b2_hbm, b3_hbm,
               xa, pos0, pos1, pos2, line0, line1, line2, sg0, sg1, sg2, sg3, dg0, dg1, dg2, dg3,
               gbuf, xv, dxb, bv, acc, w13, w2, dw13, dw2, dw1r, dw3r, dw2r,
               ld_s, ag_s, ag_r, far_s, far_r, p_s, p_r, w_s, w_r, sg_s, sg_r, dg_s, dg_r,
               s2_s, s2_r, s2_l, s3_s, s3_r, r1_s, r1_r, r1_l, r2_s, r2_r, r3_s, r3_r,
               cl_s, bl_s, dw_s, dw_r, out_s, end_s):
    tok, hidden = x_hbm.shape
    top_k = ids_ref.shape[0]
    chunks = cap // ROWS
    plane = ring * ring
    block = plane * ROWS
    send_cols = [[pl.ds(s, n) for s, n in column_groups(hidden, wide)] for wide in (2, 0)]
    cols = [pl.ds(s, n) for s, n in column_groups(hidden, 1)]
    pos = (pos0, pos1, pos2)
    line = (line0, line1, line2)
    strides = (ring * ring, ring, 1)
    me = lax.axis_index("ep")
    core = lax.axis_index("fsdp")
    other = {"fsdp": 1 - core}
    coord = [lax.rem(me // s, ring) for s in strides]
    rest = pl.ds(1, ring - 1)
    width = w1_hbm.shape[1]
    one, three = pl.ds(0, width), pl.ds(width, width)
    weights = (lambda i: w13.at[i, :, one], lambda i: w13.at[i, :, three], lambda i: w2.at[i])

    def peer(axis, d):
        c = coord[axis]
        return {"ep": me + (lax.rem(c + d, ring) - c) * strides[axis]}

    def send(src, dst, s_sem, r_sem, device):
        pltpu.make_async_remote_copy(src_ref=src, dst_ref=dst, send_sem=s_sem, recv_sem=r_sem,
                                     device_id=device, device_id_type=MESH).start()

    def expert_column(order):
        row = lax.broadcasted_iota(jnp.int32, (ring ** 3, 1), 0)
        digits = (row // (ring * ring), lax.rem(row // ring, ring), lax.rem(row, ring))
        total = jnp.zeros_like(row)
        for digit, axis in zip(digits, order):
            total = total + lax.rem(digit + coord[axis], ring) * strides[axis]
        return total

    own = [
        pltpu.make_async_copy(x_hbm, xa.at[0, 0], ld_s.at[0]),
        pltpu.make_async_copy(u_hbm, xa.at[1, 0], ld_s.at[1]),
        pltpu.make_async_copy(w1_hbm, weights[0](core), ld_s.at[2]),
        pltpu.make_async_copy(w3_hbm, weights[1](core), ld_s.at[3]),
        pltpu.make_async_copy(w2_hbm, weights[2](core), ld_s.at[4]),
    ]
    for copy in own:
        copy.start()

    barrier = pltpu.get_barrier_semaphore()
    for axis in range(3):
        for d in range(1, ring):
            pl.semaphore_signal(barrier, inc=1, device_id=peer(axis, d), device_id_type=MESH)
    pl.semaphore_signal(barrier, inc=1, device_id=other, device_id_type=MESH)

    earlier = (lax.broadcasted_iota(jnp.int32, (tok, tok), 0) < lax.broadcasted_iota(jnp.int32, (tok, tok), 1))
    earlier = jnp.where(earlier, 1.0, 0.0).astype(BF16)
    for p, order in enumerate(((0, 1, 2), (1, 0, 2), (2, 0, 1))):
        expert = expert_column(order)
        chosen = jnp.zeros((ring ** 3, tok), F32)
        for j in range(top_k):
            chosen = chosen + jnp.where(ids_ref[j:j + 1, :] == expert, 1.0, 0.0)
        before = dot(chosen.astype(BF16), earlier)
        place = jnp.where((chosen > 0.5) & (before < cap), before, -1.0)
        pos[p][...] = place.reshape(ring, plane, tok)

    pltpu.make_async_copy(pos0, pos_out, end_s.at[0]).start()
    pl.semaphore_wait(barrier, 3 * (ring - 1) + 1)

    for p in range(3):
        for d in range(1, ring):
            send(pos[p].at[d], line[p].at[ring - d], p_s.at[p], p_r.at[p], peer(p, d))

    sides = sorted({1, ring - 1})

    def gather_line(array, ref):
        for d in sides:
            for p in range(3):
                send(ref.at[:, send_cols[array][p]], xa.at[array, ring - d, :, send_cols[array][p]],
                     ag_s.at[array, p, d // 2], ag_r.at[array, p, (ring - d) // 2], peer(p, d))

    gather_line(0, x_hbm)
    gather_line(1, u_hbm)
    for i, src in enumerate((w1_hbm, w3_hbm, w2_hbm)):
        send(src, weights[i](core), w_s.at[i], w_r.at[i], other)

    expert = expert_column((0, 1, 2))
    place = pos0[...].reshape(ring ** 3, tok)
    gate = jnp.zeros((ring ** 3, tok), F32)
    for j in range(top_k):
        gate = gate + jnp.where(ids_ref[j:j + 1, :] == expert, gates_ref[j:j + 1, :], 0.0)
    lane = lax.broadcasted_iota(jnp.int32, (ring ** 3, 128), 1)

    def gate_place(i, table):
        for j in range(8):
            r = 8 * i + j
            picked = jnp.sum(jnp.where(place == r.astype(F32), gate, 0.0), axis=1, keepdims=True)
            table = jnp.where(lane == r, picked, table)
        return table

    table = lax.fori_loop(0, cap // 8, gate_place, jnp.zeros((ring ** 3, 128), F32))
    sg0[...] = table.reshape(ring, ring, ring, 1, 128)

    def small_start(axis, src, dst, s_sem, r_sem):
        sel = lambda i: tuple(i if a == axis else slice(None) for a in range(3))
        for d in range(1, ring):
            send(src.at[sel(d)], dst.at[sel(ring - d)], s_sem.at[axis], r_sem.at[axis], peer(axis, d))
        dst[sel(pl.ds(0, 1))] = src[sel(pl.ds(0, 1))]

    def small_wait(axis, dst, r_sem):
        wait_bytes(dst.at[tuple(rest if a == axis else slice(None) for a in range(3))], r_sem.at[axis])

    small_start(0, sg0, sg1, sg_s, sg_r)
    for ref in (dw13, dw2, acc, dg0):
        ref[...] = jnp.zeros_like(ref)
    for array in range(2):
        for d in sides:
            for p in range(3):
                col = send_cols[array][p]
                wait_bytes(xa.at[array, d, :, col], ag_r.at[array, p, d // 2])
                if ring == 4:
                    part = pl.ds((d // 2) * (tok // 2), tok // 2)
                    send(xa.at[array, d, part, col], xa.at[array, 2, part, col],
                         far_s.at[array, p], far_r.at[array, p], peer(p, ring - d))
    for copy in own:
        copy.wait()
    for p in range(3):
        wait_bytes(line[p].at[rest], p_r.at[p])

    def dispatch(c):
        slot = lax.rem(c, 2)
        for array in range(2):
            for p in range(3):
                axis = (p + 1) % 3

                if ring == 4:
                    @pl.when(c == 0)
                    def _():
                        wait_bytes(xa.at[array, 2, :, send_cols[array][p]], far_r.at[array, p])

                @pl.when(c >= 2)
                def _():
                    wait_bytes(at(gbuf, (array, slot), {axis: rest}, send_cols[array][p]), s2_s.at[array, slot, p])

                width = send_cols[array][p].size
                for d in range(ring):
                    places = pos[p][0] if d == 0 else line[p][d]
                    rows = dot(one_hot(places, c * ROWS), xa[array, d, :, send_cols[array][p]]).astype(BF16)
                    idx = tuple(d if a == p else slice(None) for a in range(3))
                    gbuf[(array, slot, *idx, slice(None), send_cols[array][p])] = rows.reshape(ring, ring, ROWS, width)
                for d in range(1, ring):
                    send(at(gbuf, (array, slot), {axis: d}, send_cols[array][p]),
                         at(mid_hbm, (array, c), {axis: ring - d}, send_cols[array][p]),
                         s2_s.at[array, slot, p], s2_r.at[array, c, p], peer(axis, d))
                pltpu.make_async_copy(at(gbuf, (array, slot), {axis: 0}, send_cols[array][p]),
                                      at(mid_hbm, (array, c), {axis: 0}, send_cols[array][p]), s2_l.at[array, c, p]).start()

    def forward(c):
        for array in range(2):
            for p in range(3):
                axis, last = (p + 1) % 3, (p + 2) % 3
                wait_bytes(at(mid_hbm, (array, c), {axis: rest}, send_cols[array][p]), s2_r.at[array, c, p])
                wait_bytes(at(mid_hbm, (array, c), {axis: 0}, send_cols[array][p]), s2_l.at[array, c, p])
                for d in range(1, ring):
                    send(at(mid_hbm, (array, c), {last: d}, send_cols[array][p]),
                         at(fin_hbm, (array, c), {last: ring - d}, send_cols[array][p]),
                         s3_s.at[array, c, p], s3_r.at[array, c, p], peer(last, d))

    def compute(c):
        slot = lax.rem(c, 2)
        for array in range(2):
            for p in range(3):
                last = (p + 2) % 3
                wait_bytes(at(fin_hbm, (array, c), {last: rest}, send_cols[array][p]), s3_r.at[array, c, p])
                for src, part in ((fin_hbm, rest), (mid_hbm, 0)):
                    pltpu.make_async_copy(at(src, (array, c), {last: part}, send_cols[array][p]),
                                          at(xv, (array,), {last: part}, send_cols[array][p]), cl_s.at[array, p]).start()

        @pl.when(c >= 2)
        def _():
            for p in range(3):
                wait_bytes(at(dxb, (slot,), {(p + 2) % 3: rest}, cols[p]), r1_s.at[slot, p])

        for array in range(2):
            for p in range(3):
                wait_bytes(at(xv, (array,), {}, send_cols[array][p]), cl_s.at[array, p])

        def step(i, carry):
            slabs = pl.ds(2 * i, 2)
            x = xv[0, slabs].reshape(2 * block, hidden)
            u = xv[1, slabs].reshape(2 * block, hidden)
            w13_full = w13[...].reshape(hidden, 2 * width)
            hit = (lax.broadcasted_iota(jnp.int32, (2 * plane, ROWS, 128), 2)
                   == lax.broadcasted_iota(jnp.int32, (2 * plane, ROWS, 128), 1) + c * ROWS)
            s = sg3[slabs].reshape(2 * plane, 1, 128)
            s = jnp.sum(jnp.where(hit, s, 0.0), axis=2, keepdims=True).reshape(2 * block, 1)
            h13 = dot(x, w13_full)
            h1, h3 = h13[:, :width], h13[:, width:]
            sig = jax.nn.sigmoid(h1)
            silu = h1 * sig
            act = (silu * h3).astype(BF16)
            u32 = u.astype(F32)
            g = (s * u32).astype(BF16)
            w2_full = w2[...].reshape(hidden, width)
            y = dot(act, w2_full, ((1,), (1,)))
            dg = jnp.sum(u32 * y, axis=1, keepdims=True)
            da = dot(g, w2_full)
            dw2[...] += dot(g, act, ((0,), (0,))).reshape(dw2.shape)
            dh1 = (da * h3 * sig * (1.0 + h1 * (1.0 - sig))).astype(BF16)
            dh3 = (da * silu).astype(BF16)
            dh13 = jnp.concatenate([dh1, dh3], axis=1)
            dx = dot(dh13, w13_full, ((1,), (1,)))
            dxb[slot, slabs] = dx.astype(BF16).reshape(2, ring, ring, ROWS, hidden)
            dw13[...] += dot(x, dh13, ((0,), (0,))).reshape(dw13.shape)
            spread = jnp.sum(jnp.where(hit, dg.reshape(2 * plane, ROWS, 1), 0.0), axis=1, keepdims=True)
            dg0[slabs] += spread.reshape(2, ring, ring, 1, 128)
            for j in range(2):
                return_slab(2 * i + j)
            return carry

        def return_slab(m):
            for p in range(3):
                last = (p + 2) % 3

                def start(here, there, device):
                    src, dst = at(dxb, (slot,), here, cols[p]), at(b1_hbm, (c,), there, cols[p])
                    if device is None:
                        pltpu.make_async_copy(src, dst, r1_l.at[c, p]).start()
                    else:
                        send(src, dst, r1_s.at[slot, p], r1_r.at[c, p], device)

                if last == 0:
                    @pl.when(m > 0)
                    def _():
                        start({0: m}, {0: ring - m}, peer(0, m))

                    @pl.when(m == 0)
                    def _():
                        start({0: 0}, {0: 0}, None)
                else:
                    for d in range(1, ring):
                        start({0: m, last: d}, {0: m, last: ring - d}, peer(last, d))
                    start({0: m, last: 0}, {0: m, last: 0}, None)

        lax.fori_loop(0, ring // 2, step, 0)

    def back_two(c):
        for p in range(3):
            axis, last = (p + 1) % 3, (p + 2) % 3
            wait_bytes(at(b1_hbm, (c,), {last: rest}, cols[p]), r1_r.at[c, p])
            wait_bytes(at(b1_hbm, (c,), {last: 0}, cols[p]), r1_l.at[c, p])
            for d in range(1, ring):
                send(at(b1_hbm, (c,), {axis: d}, cols[p]), at(b2_hbm, (c,), {axis: ring - d}, cols[p]),
                     r2_s.at[c, p], r2_r.at[c, p], peer(axis, d))

    def back_three(c):
        for p in range(3):
            axis = (p + 1) % 3
            wait_bytes(at(b2_hbm, (c,), {axis: rest}, cols[p]), r2_r.at[c, p])
            for d in range(1, ring):
                for src, part in ((b2_hbm, rest), (b1_hbm, 0)):
                    send(at(src, (c,), {p: d, axis: part}, cols[p]),
                         at(b3_hbm, (c,), {p: ring - d, axis: part}, cols[p]),
                         r3_s.at[c, p], r3_r.at[c, p], peer(p, d))

    def combine(c):
        for p in range(3):
            wait_bytes(at(b3_hbm, (c,), {p: rest}, cols[p]), r3_r.at[c, p])
            for src, sel in zip((b1_hbm, b2_hbm, b3_hbm), returned_parts(ring, p)):
                pltpu.make_async_copy(at(src, (c,), sel, cols[p]), at(bv, (), sel, cols[p]), bl_s.at[p]).start()
        for p in range(3):
            wait_bytes(at(bv, (), {}, cols[p]), bl_s.at[p])

        def step(m, carry):
            acc[...] += dot(one_hot(pos0[m], c * ROWS), bv[m].reshape(block, hidden), ((0,), (0,)))
            return carry

        lax.fori_loop(0, ring, step, 0)

    grads = (
        (lambda i: dw13.at[i, :, one], dw1r, g1_out),
        (lambda i: dw13.at[i, :, three], dw3r, g3_out),
        (lambda i: dw2.at[i], dw2r, g2_out),
    )

    def gate_grads():
        small_wait(0, dg3, dg_r)
        expert = expert_column((0, 1, 2))
        place = pos0[...].reshape(ring ** 3, tok)
        values = dg3[...].reshape(ring ** 3, 128)

        def pick(i, total):
            for j in range(8):
                r = 8 * i + j
                value = jnp.sum(jnp.where(lane == r, values, 0.0), axis=1, keepdims=True)
                total = total + jnp.where(place == r.astype(F32), value, 0.0)
            return total

        dense = lax.fori_loop(0, cap // 8, pick, jnp.zeros((ring ** 3, tok), F32))
        for j in range(top_k):
            dg_out[j:j + 1, :] = jnp.sum(jnp.where(ids_ref[j:j + 1, :] == expert, dense, 0.0), axis=0, keepdims=True)

    def tick(k, carry):
        @pl.when(k < chunks)
        def _():
            dispatch(k)

        @pl.when(k == 0)
        def _():
            small_wait(0, sg1, sg_r)
            small_start(1, sg1, sg2, sg_s, sg_r)

        @pl.when(k == 1)
        def _():
            small_wait(1, sg2, sg_r)
            small_start(2, sg2, sg3, sg_s, sg_r)

        @pl.when((k >= 1) & (k <= chunks))
        def _():
            forward(k - 1)

        @pl.when(k == 2)
        def _():
            small_wait(2, sg3, sg_r)
            for i in range(3):
                wait_bytes(weights[i](1 - core), w_r.at[i])

        @pl.when(k >= 2)
        def _():
            compute(k - 2)

        @pl.when(k >= 3)
        def _():
            back_two(k - 3)

        @pl.when(k >= 4)
        def _():
            back_three(k - 4)

        @pl.when((k >= 5) & (k <= chunks))
        def _():
            combine(k - 5)

        return carry

    lax.fori_loop(0, chunks + 2, tick, 0)
    last_one = chunks - 1
    small_start(2, dg0, dg1, dg_s, dg_r)
    for i, (mine, theirs, _) in enumerate(grads):
        send(mine(1 - core), theirs, dw_s.at[i], dw_r.at[i], other)
    back_two(last_one)
    combine(last_one - 3)
    back_three(last_one - 1)
    small_wait(2, dg1, dg_r)
    small_start(1, dg1, dg2, dg_s, dg_r)
    combine(last_one - 2)
    back_three(last_one)
    small_wait(1, dg2, dg_r)
    small_start(0, dg2, dg3, dg_s, dg_r)
    for i, (mine, theirs, out) in enumerate(grads):
        wait_bytes(theirs, dw_r.at[i])
        theirs[...] += mine(core)[...]
        pltpu.make_async_copy(theirs, out, out_s.at[i]).start()
    combine(last_one - 1)
    pltpu.make_async_copy(acc, acc_out, end_s.at[1]).start()
    gate_grads()

    for array in range(2):
        for p in range(3):
            for d in sides:
                wait_bytes(xa.at[array, d, :, send_cols[array][p]], ag_s.at[array, p, d // 2])
            if ring == 4:
                wait_bytes(xa.at[array, 2, :, send_cols[array][p]], far_s.at[array, p])
    for p in range(3):
        wait_bytes(line[p].at[rest], p_s.at[p])
        wait_bytes(sg1.at[rest], sg_s.at[p])
        wait_bytes(dg1.at[rest], dg_s.at[p])
    for i in range(3):
        wait_bytes(weights[i](1 - core), w_s.at[i])
    for i, (mine, theirs, out) in enumerate(grads):
        wait_bytes(theirs, dw_s.at[i])
        wait_bytes(out, out_s.at[i])
    for slot in range(2):
        for p in range(3):
            axis, last = (p + 1) % 3, (p + 2) % 3
            for array in range(2):
                wait_bytes(at(gbuf, (array, slot), {axis: rest}, send_cols[array][p]), s2_s.at[array, slot, p])
            wait_bytes(at(dxb, (slot,), {last: rest}, cols[p]), r1_s.at[slot, p])

    def drain(c, carry):
        for p in range(3):
            axis, last = (p + 1) % 3, (p + 2) % 3
            for array in range(2):
                wait_bytes(at(fin_hbm, (array, c), {last: rest}, send_cols[array][p]), s3_s.at[array, c, p])
            wait_bytes(at(b2_hbm, (c,), {axis: rest}, cols[p]), r2_s.at[c, p])
            wait_bytes(at(b3_hbm, (c,), {p: rest}, cols[p]), r3_s.at[c, p])
        return carry

    lax.fori_loop(0, chunks, drain, 0)
    wait_bytes(pos_out, end_s.at[0])
    wait_bytes(acc_out, end_s.at[1])
    for p in range(3):
        wait_bytes(at(b3_hbm, (last_one,), {p: rest}, cols[p]), r3_r.at[last_one, p])


def finish_kernel(ring, cap, acc_hbm, pos_hbm, g1_hbm, g3_hbm, g2_hbm, b1_hbm, b2_hbm, b3_hbm,
                  dx_hbm, g1_out, g3_out, g2_out, acc, pos, grad, bv, dx, in_s, out_s):
    hidden = acc.shape[1]
    chunk = cap // ROWS - 1
    cols = [pl.ds(s, n) for s, n in column_groups(hidden, 1)]
    pltpu.make_async_copy(pos_hbm, pos, in_s.at[0]).start()
    for p in range(3):
        for src, sel in zip((b1_hbm, b2_hbm, b3_hbm), returned_parts(ring, p)):
            pltpu.make_async_copy(at(src, (chunk,), sel, cols[p]), at(bv, (), sel, cols[p]), in_s.at[1]).start()
    pltpu.make_async_copy(acc_hbm, acc, in_s.at[2]).start()
    for i, src in enumerate((g1_hbm, g3_hbm, g2_hbm)):
        pltpu.make_async_copy(src, grad.at[i], in_s.at[3 + i]).start()
    wait_bytes(pos, in_s.at[0])
    wait_bytes(bv, in_s.at[1])
    wait_bytes(acc, in_s.at[2])
    for m in range(ring):
        block = ring * ring * ROWS
        acc[...] += dot(one_hot(pos[m], chunk * ROWS), bv[m].reshape(block, hidden), ((0,), (0,)))
        if m < 3:
            wait_bytes(grad.at[m], in_s.at[3 + m])
            pltpu.make_async_copy(grad.at[m], (g1_out, g3_out, g2_out)[m], out_s.at[m]).start()
    for m in range(ring, 3):
        wait_bytes(grad.at[m], in_s.at[3 + m])
        pltpu.make_async_copy(grad.at[m], (g1_out, g3_out, g2_out)[m], out_s.at[m]).start()
    dx[...] = acc[...].astype(BF16)
    copy = pltpu.make_async_copy(dx, dx_hbm, out_s.at[3])
    copy.start()
    for m, out in enumerate((g1_out, g3_out, g2_out)):
        wait_bytes(out, out_s.at[m])
    copy.wait()


def build(mesh, capacity=None):
    ep_size = mesh.shape["ep"]
    ring = round(ep_size ** (1 / 3))
    tok_spec = P(("fsdp", "ep"), None)
    up_spec = P("ep", "fsdp", None)
    down_spec = P("ep", None, "fsdp")

    def per_device(layer_in, out_grad, expert_ids, gate_vals, w_one, w_two, w_three):
        tok, hidden = layer_in.shape
        top_k = expert_ids.shape[1]
        _, half, width = w_one.shape
        cap = capacity or capacity_of(tok, top_k, ep_size)
        chunks = cap // ROWS
        cube = (ring, ring, ring, ROWS, hidden)
        table = (ring, ring * ring, tok)
        small = (ring, ring, ring, 1, 128)
        vmem, dma = pltpu.VMEM, pltpu.SemaphoreType.DMA
        hbm = pl.BlockSpec(memory_space=pl.ANY)
        local = pl.BlockSpec(memory_space=pltpu.VMEM)
        sds = jax.ShapeDtypeStruct
        outs = pl.pallas_call(
            functools.partial(moe_kernel, ring, cap),
            out_shape=[
                sds((top_k, tok), F32), sds((tok, hidden), F32), sds(table, F32),
                *[sds((half, width), F32)] * 3,
                sds((2, chunks, *cube), BF16), sds((2, chunks, *cube), BF16),
                sds((chunks, *cube), BF16), sds((chunks, *cube), BF16), sds((chunks, *cube), BF16),
            ],
            in_specs=[hbm, hbm, local, local, hbm, hbm, hbm],
            out_specs=[local] + [hbm] * 10,
            scratch_shapes=[
                vmem((2, ring, tok, hidden), BF16),
                *[vmem(table, F32)] * 6,
                *[vmem(small, F32)] * 8,
                vmem((2, 2, *cube), BF16), vmem((2, *cube), BF16), vmem((2, *cube), BF16), vmem(cube, BF16),
                vmem((tok, hidden), F32),
                vmem((2, half, 2 * width), BF16), vmem((2, half, width), BF16),
                vmem((2, half, 2 * width), F32), vmem((2, half, width), F32),
                *[vmem((half, width), F32)] * 3,
                dma((5,)), dma((2, 3, 2)), dma((2, 3, 2)), dma((2, 3)), dma((2, 3)), dma((3,)), dma((3,)), dma((3,)), dma((3,)),
                dma((3,)), dma((3,)), dma((3,)), dma((3,)),
                dma((2, 2, 3)), dma((2, chunks, 3)), dma((2, chunks, 3)),
                dma((2, chunks, 3)), dma((2, chunks, 3)),
                dma((2, 3)), dma((chunks, 3)), dma((chunks, 3)),
                dma((chunks, 3)), dma((chunks, 3)), dma((chunks, 3)), dma((chunks, 3)),
                dma((2, 3)), dma((3,)), dma((3,)), dma((3,)), dma((3,)), dma((2,)),
            ],
            compiler_params=pltpu.CompilerParams(
                collective_id=0, has_side_effects=True, vmem_limit_bytes=63 << 20
            ),
            name="moe_backward",
        )(layer_in, out_grad, expert_ids.T, gate_vals.T, w_one[0], w_three[0], w_two[0].T)
        dg, acc, places, g1, g3, g2 = outs[:6]
        dx, g1, g3, g2 = pl.pallas_call(
            functools.partial(finish_kernel, ring, cap),
            out_shape=[sds((tok, hidden), BF16), *[sds((half, width), F32)] * 3],
            in_specs=[hbm] * 8,
            out_specs=[hbm] * 4,
            scratch_shapes=[
                vmem((tok, hidden), F32), vmem(table, F32), vmem((3, half, width), F32), vmem(cube, BF16),
                vmem((tok, hidden), BF16), dma((6,)), dma((4,)),
            ],
            compiler_params=pltpu.CompilerParams(vmem_limit_bytes=63 << 20),
            name="moe_finish",
        )(acc, places, g1, g3, g2, *outs[8:])
        return dx, dg.T, g1[None], g2.T[None], g3[None]

    return jax.shard_map(per_device, mesh=mesh,
                         in_specs=(tok_spec, tok_spec, tok_spec, tok_spec, up_spec, down_spec, up_spec),
                         out_specs=(tok_spec, tok_spec, up_spec, down_spec, up_spec), check_vma=False)


def solution(mesh):
    return build(mesh)
```

time: 311 us -> 281 us (0.904)
  Pallas kernels: 301 us -> 279 us
  local copies, waits for them, and re-layouts: 8.54 us -> 0.61 us
    pallas_call x1, Pallas kernels: 301 us -> 274 us  [per_device(): pl.pallas_call(functools.partial(moe_kernel, ring, cap), out_shape=[sds((...]
    unnamed x14 -> x3, local copies, waits for them, and re-layouts: 8.54 us -> 0.61 us
    pallas_call x0 -> x1, Pallas kernels: none -> 4.76 us  [per_device(): pl.pallas_call(functools.partial(finish_kernel, ring, cap), out_shape=[sd...]
where the time goes in v2:
time: 281 us; the launch traced here: 280 us
  Pallas kernels  279 us (99%)
    pallas_call x1, Pallas kernels, per_device(): pl.pallas_call(functools.partial(moe_kernel, ring, cap), out_shape=[sds((...  274 us

profile of v2, /device:TPU:0, one launch (start us, length us, event | category | flops | bytes accessed | tf_op | source)
XLA Modules:
  0.0 280.1 jit_solution(6234725854729878137)
XLA Ops:
  0.6 274.1 %moe_backward.1 = (f32[8,512]{1,0:T(8,128)}, f32[512,896]{1,0:T(8,128)}, f32[4,16,512]{2,1,0:T(8,128)}, f32[448,640]{1,0:T(8,128)}, f32[448,640]{1,0:T(8,128)}, ...) custom-call(bf16[512,896]{1,0:T(8,128)(2,1)} %x_hbm.1, ...), custom_call_target="tpu_custom_call" | custom-call | tf_op jit(solution)/shard_map/moe_backward/pallas_call | solution.py:512
  274.7 0.0 copy-start
  274.7 4.8 %moe_finish.1 = (bf16[512,896]{1,0:T(8,128)(2,1)}, f32[448,640]{1,0:T(8,128)}, f32[448,640]{1,0:T(8,128)}, f32[448,640]{1,0:T(8,128)}) custom-call(f32[512,896]{1,0:T(8,128)} %get-tuple-element.18.acc_hbm, f32[4,16,512]{2,1,0:T(8,128)} %get-tuple-element.19.pos_hbm, f32[448,640]{1,0:T(8,128)} %get-tuple-element.20.g1_hbm, ...), custom_call_target="tpu_custom_call" | custom-call | tf_op jit(solution)/shard_map/moe_finish/pallas_call | solution.py:545
  279.5 0.0 copy-done
  279.5 0.6 copy.13
Async XLA Ops:
  274.7 4.8 %copy-start = (f32[8,512]{1,0:T(8,128)S(1)}, f32[8,512]{1,0:T(8,128)}, u32[]{:S(2)}) copy-start(f32[8,512]{1,0:T(8,128)} %get-tuple-element.27) | copy-start | bytes 49156

commit v3 on v2

--- a/solution.py
+++ b/solution.py
@@ -25,6 +25,13 @@
     return [(128 * s, 128 * n) for s, n in zip(starts, sizes)]
 
 
+def split_groups(width):
+    base, spare = width // 384 * 128, width % 384
+    even = [(0, base), (base, base), (2 * base, spare + base)]
+    odd = [(0, base), (base, base + spare), (2 * base + spare, base)]
+    return even, odd, (2 * base, spare)
+
+
 def wait_bytes(ref, sem):
     pltpu.make_async_copy(ref, ref, sem).wait()
 
@@ -51,7 +58,7 @@
 
 def moe_kernel(ring, cap, x_hbm, u_hbm, ids_ref, gates_ref, w1_hbm, w3_hbm, w2_hbm,
                dg_out, acc_out, pos_out, g1_out, g3_out, g2_out, mid_hbm, fin_hbm, b1_hbm, b2_hbm, b3_hbm,
-               xa, pos0, pos1, pos2, line0, line1, line2, sg0, sg1, sg2, sg3, dg0, dg1, dg2, dg3,
+               xa, xe, pos0, pos1, pos2, line0, line1, line2, sg0, sg1, sg2, sg3, dg0, dg1, dg2, dg3,
                gbuf, xv, dxb, bv, acc, w13, w2, dw13, dw2, dw1r, dw3r, dw2r,
                ld_s, ag_s, ag_r, far_s, far_r, p_s, p_r, w_s, w_r, sg_s, sg_r, dg_s, dg_r,
                s2_s, s2_r, s2_l, s3_s, s3_r, r1_s, r1_r, r1_l, r2_s, r2_r, r3_s, r3_r,
@@ -61,8 +68,25 @@
     chunks = cap // ROWS
     plane = ring * ring
     block = plane * ROWS
-    send_cols = [[pl.ds(s, n) for s, n in column_groups(hidden, wide)] for wide in (2, 0)]
-    cols = [pl.ds(s, n) for s, n in column_groups(hidden, 1)]
+    even, odd, spare = split_groups(hidden)
+    spans = lambda groups: [pl.ds(s, n) for s, n in groups]
+    even, odd, u_cols, cols = spans(even), spans(odd), spans(column_groups(hidden, 0)), spans(column_groups(hidden, 1))
+    spare = pl.ds(*spare)
+    pieces = [(0, 0, even[0]), (0, 1, even[1]), (0, 2, even[2])] + ([(0, 1, spare)] if spare.size else [])
+    pieces += [(1, p, u_cols[p]) for p in range(3)]
+
+    def held(i, d, part=slice(None), col=None):
+        array, axis, whole = pieces[i]
+        return xe.at[d, part] if i == 3 and spare.size else xa.at[array, d, part, col or whole]
+
+    def by_chunk(array, c, body):
+        if array == 1:
+            body(u_cols)
+        elif isinstance(c, int):
+            body(odd if c % 2 else even)
+        else:
+            for parity, groups in enumerate((even, odd)):
+                pl.when(lax.rem(c, 2) == parity)(functools.partial(body, groups))
     pos = (pos0, pos1, pos2)
     line = (line0, line1, line2)
     strides = (ring * ring, ring, 1)
@@ -94,6 +118,7 @@
     own = [
         pltpu.make_async_copy(x_hbm, xa.at[0, 0], ld_s.at[0]),
         pltpu.make_async_copy(u_hbm, xa.at[1, 0], ld_s.at[1]),
+        *([pltpu.make_async_copy(x_hbm.at[:, spare], xe.at[0], ld_s.at[5])] if spare.size else []),
         pltpu.make_async_copy(w1_hbm, weights[0](core), ld_s.at[2]),
         pltpu.make_async_copy(w3_hbm, weights[1](core), ld_s.at[3]),
         pltpu.make_async_copy(w2_hbm, weights[2](core), ld_s.at[4]),
@@ -127,14 +152,10 @@
 
     sides = sorted({1, ring - 1})
 
-    def gather_line(array, ref):
+    for i, (array, axis, col) in enumerate(pieces):
         for d in sides:
-            for p in range(3):
-                send(ref.at[:, send_cols[array][p]], xa.at[array, ring - d, :, send_cols[array][p]],
-                     ag_s.at[array, p, d // 2], ag_r.at[array, p, (ring - d) // 2], peer(p, d))
-
-    gather_line(0, x_hbm)
-    gather_line(1, u_hbm)
+            send((x_hbm, u_hbm)[array].at[:, col], held(i, ring - d), ag_s.at[i, d // 2], ag_r.at[i, (ring - d) // 2],
+                 peer(axis, d))
     for i, src in enumerate((w1_hbm, w3_hbm, w2_hbm)):
         send(src, weights[i](core), w_s.at[i], w_r.at[i], other)
 
@@ -167,68 +188,78 @@
     small_start(0, sg0, sg1, sg_s, sg_r)
     for ref in (dw13, dw2, acc, dg0):
         ref[...] = jnp.zeros_like(ref)
-    for array in range(2):
+    for i, (array, axis, col) in enumerate(pieces):
         for d in sides:
-            for p in range(3):
-                col = send_cols[array][p]
-                wait_bytes(xa.at[array, d, :, col], ag_r.at[array, p, d // 2])
-                if ring == 4:
-                    part = pl.ds((d // 2) * (tok // 2), tok // 2)
-                    send(xa.at[array, d, part, col], xa.at[array, 2, part, col],
-                         far_s.at[array, p], far_r.at[array, p], peer(p, ring - d))
+            wait_bytes(held(i, d), ag_r.at[i, d // 2])
+            if ring == 4:
+                part = pl.ds((d // 2) * (tok // 2), tok // 2)
+                send(held(i, d, part), held(i, 2, part), far_s.at[i], far_r.at[i], peer(axis, ring - d))
     for copy in own:
         copy.wait()
     for p in range(3):
         wait_bytes(line[p].at[rest], p_r.at[p])
 
     def dispatch(c):
+        for array in range(2):
+            by_chunk(array, c, functools.partial(dispatch_stream, c, array))
+
+    def dispatch_stream(c, array, groups):
         slot = lax.rem(c, 2)
-        for array in range(2):
-            for p in range(3):
-                axis = (p + 1) % 3
-
+        for p in range(3):
+            axis, col = (p + 1) % 3, groups[p]
+            mine = [i for i, piece in enumerate(pieces) if piece[:2] == (array, p)]
+            for i in mine:
                 if ring == 4:
                     @pl.when(c == 0)
                     def _():
-                        wait_bytes(xa.at[array, 2, :, send_cols[array][p]], far_r.at[array, p])
-
-                @pl.when(c >= 2)
-                def _():
-                    wait_bytes(at(gbuf, (array, slot), {axis: rest}, send_cols[array][p]), s2_s.at[array, slot, p])
-
-                width = send_cols[array][p].size
-                for d in range(ring):
-                    places = pos[p][0] if d == 0 else line[p][d]
-                    rows = dot(one_hot(places, c * ROWS), xa[array, d, :, send_cols[array][p]]).astype(BF16)
+                        wait_bytes(held(i, 2), far_r.at[i])
+
+            @pl.when(c >= 2)
+            def _():
+                wait_bytes(at(gbuf, (array, slot), {axis: rest}, col), s2_s.at[array, slot, p])
+
+            for d in range(ring):
+                hot = one_hot(pos[p][0] if d == 0 else line[p][d], c * ROWS)
+                for i in mine:
+                    first = max(pieces[i][2].start, col.start)
+                    end = min(pieces[i][2].start + pieces[i][2].size, col.start + col.size)
+                    if first >= end:
+                        continue
+                    own_col = pl.ds(first, end - first)
+                    rows = dot(hot, held(i, d, col=own_col)[...]).astype(BF16)
                     idx = tuple(d if a == p else slice(None) for a in range(3))
-                    gbuf[(array, slot, *idx, slice(None), send_cols[array][p])] = rows.reshape(ring, ring, ROWS, width)
-                for d in range(1, ring):
-                    send(at(gbuf, (array, slot), {axis: d}, send_cols[array][p]),
-                         at(mid_hbm, (array, c), {axis: ring - d}, send_cols[array][p]),
-                         s2_s.at[array, slot, p], s2_r.at[array, c, p], peer(axis, d))
-                pltpu.make_async_copy(at(gbuf, (array, slot), {axis: 0}, send_cols[array][p]),
-                                      at(mid_hbm, (array, c), {axis: 0}, send_cols[array][p]), s2_l.at[array, c, p]).start()
+                    gbuf[(array, slot, *idx, slice(None), own_col)] = rows.reshape(ring, ring, ROWS, own_col.size)
+            for d in range(1, ring):
+                send(at(gbuf, (array, slot), {axis: d}, col), at(mid_hbm, (array, c), {axis: ring - d}, col),
+                     s2_s.at[array, slot, p], s2_r.at[array, c, p], peer(axis, d))
+            pltpu.make_async_copy(at(gbuf, (array, slot), {axis: 0}, col),
+                                  at(mid_hbm, (array, c), {axis: 0}, col), s2_l.at[array, c, p]).start()
 
     def forward(c):
         for array in range(2):
-            for p in range(3):
-                axis, last = (p + 1) % 3, (p + 2) % 3
-                wait_bytes(at(mid_hbm, (array, c), {axis: rest}, send_cols[array][p]), s2_r.at[array, c, p])
-                wait_bytes(at(mid_hbm, (array, c), {axis: 0}, send_cols[array][p]), s2_l.at[array, c, p])
-                for d in range(1, ring):
-                    send(at(mid_hbm, (array, c), {last: d}, send_cols[array][p]),
-                         at(fin_hbm, (array, c), {last: ring - d}, send_cols[array][p]),
-                         s3_s.at[array, c, p], s3_r.at[array, c, p], peer(last, d))
+            by_chunk(array, c, functools.partial(forward_stream, c, array))
+
+    def forward_stream(c, array, groups):
+        for p, col in enumerate(groups):
+            axis, last = (p + 1) % 3, (p + 2) % 3
+            wait_bytes(at(mid_hbm, (array, c), {axis: rest}, col), s2_r.at[array, c, p])
+            wait_bytes(at(mid_hbm, (array, c), {axis: 0}, col), s2_l.at[array, c, p])
+            for d in range(1, ring):
+                send(at(mid_hbm, (array, c), {last: d}, col), at(fin_hbm, (array, c), {last: ring - d}, col),
+                     s3_s.at[array, c, p], s3_r.at[array, c, p], peer(last, d))
+
+    def load_stream(c, array, groups):
+        for p, col in enumerate(groups):
+            last = (p + 2) % 3
+            wait_bytes(at(fin_hbm, (array, c), {last: rest}, col), s3_r.at[array, c, p])
+            for src, part in ((fin_hbm, rest), (mid_hbm, 0)):
+                pltpu.make_async_copy(at(src, (array, c), {last: part}, col),
+                                      at(xv, (array,), {last: part}, col), cl_s.at[array]).start()
 
     def compute(c):
         slot = lax.rem(c, 2)
         for array in range(2):
-            for p in range(3):
-                last = (p + 2) % 3
-                wait_bytes(at(fin_hbm, (array, c), {last: rest}, send_cols[array][p]), s3_r.at[array, c, p])
-                for src, part in ((fin_hbm, rest), (mid_hbm, 0)):
-                    pltpu.make_async_copy(at(src, (array, c), {last: part}, send_cols[array][p]),
-                                          at(xv, (array,), {last: part}, send_cols[array][p]), cl_s.at[array, p]).start()
+            by_chunk(array, c, functools.partial(load_stream, c, array))
 
         @pl.when(c >= 2)
         def _():
@@ -236,8 +267,7 @@
                 wait_bytes(at(dxb, (slot,), {(p + 2) % 3: rest}, cols[p]), r1_s.at[slot, p])
 
         for array in range(2):
-            for p in range(3):
-                wait_bytes(at(xv, (array,), {}, send_cols[array][p]), cl_s.at[array, p])
+            wait_bytes(xv.at[array], cl_s.at[array])
 
         def step(i, carry):
             slabs = pl.ds(2 * i, 2)
@@ -419,12 +449,11 @@
     pltpu.make_async_copy(acc, acc_out, end_s.at[1]).start()
     gate_grads()
 
-    for array in range(2):
-        for p in range(3):
-            for d in sides:
-                wait_bytes(xa.at[array, d, :, send_cols[array][p]], ag_s.at[array, p, d // 2])
-            if ring == 4:
-                wait_bytes(xa.at[array, 2, :, send_cols[array][p]], far_s.at[array, p])
+    for i in range(len(pieces)):
+        for d in sides:
+            wait_bytes(held(i, d), ag_s.at[i, d // 2])
+        if ring == 4:
+            wait_bytes(held(i, 2), far_s.at[i])
     for p in range(3):
         wait_bytes(line[p].at[rest], p_s.at[p])
         wait_bytes(sg1.at[rest], sg_s.at[p])
@@ -438,14 +467,16 @@
         for p in range(3):
             axis, last = (p + 1) % 3, (p + 2) % 3
             for array in range(2):
-                wait_bytes(at(gbuf, (array, slot), {axis: rest}, send_cols[array][p]), s2_s.at[array, slot, p])
+                by_chunk(array, slot, lambda groups: wait_bytes(
+                    at(gbuf, (array, slot), {axis: rest}, groups[p]), s2_s.at[array, slot, p]))
             wait_bytes(at(dxb, (slot,), {last: rest}, cols[p]), r1_s.at[slot, p])
 
     def drain(c, carry):
         for p in range(3):
             axis, last = (p + 1) % 3, (p + 2) % 3
             for array in range(2):
-                wait_bytes(at(fin_hbm, (array, c), {last: rest}, send_cols[array][p]), s3_s.at[array, c, p])
+                by_chunk(array, c, lambda groups: wait_bytes(
+                    at(fin_hbm, (array, c), {last: rest}, groups[p]), s3_s.at[array, c, p]))
             wait_bytes(at(b2_hbm, (c,), {axis: rest}, cols[p]), r2_s.at[c, p])
             wait_bytes(at(b3_hbm, (c,), {p: rest}, cols[p]), r3_s.at[c, p])
         return carry
@@ -457,8 +488,8 @@
         wait_bytes(at(b3_hbm, (last_one,), {p: rest}, cols[p]), r3_r.at[last_one, p])
 
 
-def finish_kernel(ring, cap, acc_hbm, pos_hbm, g1_hbm, g3_hbm, g2_hbm, b1_hbm, b2_hbm, b3_hbm,
-                  dx_hbm, g1_out, g3_out, g2_out, acc, pos, grad, bv, dx, in_s, out_s):
+def finish_kernel(ring, cap, dg_hbm, acc_hbm, pos_hbm, g1_hbm, g3_hbm, g2_hbm, b1_hbm, b2_hbm, b3_hbm,
+                  dx_hbm, dg_out, g1_out, g3_out, g2_out, acc, pos, grad, bv, dx, dg, in_s, out_s):
     hidden = acc.shape[1]
     chunk = cap // ROWS - 1
     cols = [pl.ds(s, n) for s, n in column_groups(hidden, 1)]
@@ -469,6 +500,7 @@
     pltpu.make_async_copy(acc_hbm, acc, in_s.at[2]).start()
     for i, src in enumerate((g1_hbm, g3_hbm, g2_hbm)):
         pltpu.make_async_copy(src, grad.at[i], in_s.at[3 + i]).start()
+    pltpu.make_async_copy(dg_hbm, dg, in_s.at[6]).start()
     wait_bytes(pos, in_s.at[0])
     wait_bytes(bv, in_s.at[1])
     wait_bytes(acc, in_s.at[2])
@@ -481,11 +513,14 @@
     for m in range(ring, 3):
         wait_bytes(grad.at[m], in_s.at[3 + m])
         pltpu.make_async_copy(grad.at[m], (g1_out, g3_out, g2_out)[m], out_s.at[m]).start()
+    wait_bytes(dg, in_s.at[6])
+    pltpu.make_async_copy(dg, dg_out, out_s.at[4]).start()
     dx[...] = acc[...].astype(BF16)
     copy = pltpu.make_async_copy(dx, dx_hbm, out_s.at[3])
     copy.start()
     for m, out in enumerate((g1_out, g3_out, g2_out)):
         wait_bytes(out, out_s.at[m])
+    wait_bytes(dg_out, out_s.at[4])
     copy.wait()
 
 
@@ -520,7 +555,7 @@
             in_specs=[hbm, hbm, local, local, hbm, hbm, hbm],
             out_specs=[local] + [hbm] * 10,
             scratch_shapes=[
-                vmem((2, ring, tok, hidden), BF16),
+                vmem((2, ring, tok, hidden), BF16), vmem((ring, tok, 128), BF16),
                 *[vmem(table, F32)] * 6,
                 *[vmem(small, F32)] * 8,
                 vmem((2, 2, *cube), BF16), vmem((2, *cube), BF16), vmem((2, *cube), BF16), vmem(cube, BF16),
@@ -528,13 +563,13 @@
                 vmem((2, half, 2 * width), BF16), vmem((2, half, width), BF16),
                 vmem((2, half, 2 * width), F32), vmem((2, half, width), F32),
                 *[vmem((half, width), F32)] * 3,
-                dma((5,)), dma((2, 3, 2)), dma((2, 3, 2)), dma((2, 3)), dma((2, 3)), dma((3,)), dma((3,)), dma((3,)), dma((3,)),
+                dma((6,)), dma((7, 2)), dma((7, 2)), dma((7,)), dma((7,)), dma((3,)), dma((3,)), dma((3,)), dma((3,)),
                 dma((3,)), dma((3,)), dma((3,)), dma((3,)),
                 dma((2, 2, 3)), dma((2, chunks, 3)), dma((2, chunks, 3)),
                 dma((2, chunks, 3)), dma((2, chunks, 3)),
                 dma((2, 3)), dma((chunks, 3)), dma((chunks, 3)),
                 dma((chunks, 3)), dma((chunks, 3)), dma((chunks, 3)), dma((chunks, 3)),
-                dma((2, 3)), dma((3,)), dma((3,)), dma((3,)), dma((3,)), dma((2,)),
+                dma((2,)), dma((3,)), dma((3,)), dma((3,)), dma((3,)), dma((2,)),
             ],
             compiler_params=pltpu.CompilerParams(
                 collective_id=0, has_side_effects=True, vmem_limit_bytes=63 << 20
@@ -542,18 +577,18 @@
             name="moe_backward",
         )(layer_in, out_grad, expert_ids.T, gate_vals.T, w_one[0], w_three[0], w_two[0].T)
         dg, acc, places, g1, g3, g2 = outs[:6]
-        dx, g1, g3, g2 = pl.pallas_call(
+        dx, dg, g1, g3, g2 = pl.pallas_call(
             functools.partial(finish_kernel, ring, cap),
-            out_shape=[sds((tok, hidden), BF16), *[sds((half, width), F32)] * 3],
-            in_specs=[hbm] * 8,
-            out_specs=[hbm] * 4,
+            out_shape=[sds((tok, hidden), BF16), sds((top_k, tok), F32), *[sds((half, width), F32)] * 3],
+            in_specs=[hbm] * 9,
+            out_specs=[hbm] * 5,
             scratch_shapes=[
                 vmem((tok, hidden), F32), vmem(table, F32), vmem((3, half, width), F32), vmem(cube, BF16),
-                vmem((tok, hidden), BF16), dma((6,)), dma((4,)),
+                vmem((tok, hidden), BF16), vmem((top_k, tok), F32), dma((7,)), dma((5,)),
             ],
             compiler_params=pltpu.CompilerParams(vmem_limit_bytes=63 << 20),
             name="moe_finish",
-        )(acc, places, g1, g3, g2, *outs[8:])
+        )(dg, acc, places, g1, g3, g2, *outs[8:])
         return dx, dg.T, g1[None], g2.T[None], g3[None]
 
     return jax.shard_map(per_device, mesh=mesh,

time: 281 us -> 275 us (0.979)
  Pallas kernels: 279 us -> 274 us
    pallas_call x1, Pallas kernels: 274 us -> 269 us  [per_device(): pl.pallas_call(functools.partial(moe_kernel, ring, cap), out_shape=[sds((...]
where the time goes in v3:
time: 275 us; the launch traced here: 274 us
  Pallas kernels  274 us (100%)
    pallas_call x1, Pallas kernels, per_device(): pl.pallas_call(functools.partial(moe_kernel, ring, cap), out_shape=[sds((...  269 us

profile of v3, /device:TPU:0, one launch (start us, length us, event | category | flops | bytes accessed | tf_op | source)
XLA Modules:
  0.0 274.5 jit_solution(13302287675604575420)
XLA Ops:
  0.6 268.8 %moe_backward.1 = (f32[8,512]{1,0:T(8,128)}, f32[512,896]{1,0:T(8,128)}, f32[4,16,512]{2,1,0:T(8,128)}, f32[448,640]{1,0:T(8,128)}, f32[448,640]{1,0:T(8,128)}, ...) custom-call(bf16[512,896]{1,0:T(8,128)(2,1)} %x_hbm.1, ...), custom_call_target="tpu_custom_call" | custom-call | tf_op jit(solution)/shard_map/moe_backward/pallas_call | solution.py:547
  269.5 4.9 %moe_finish.1 = (bf16[512,896]{1,0:T(8,128)(2,1)}, f32[8,512]{1,0:T(8,128)}, f32[448,640]{1,0:T(8,128)}, f32[448,640]{1,0:T(8,128)}, f32[448,640]{1,0:T(8,128)}) custom-call(f32[8,512]{1,0:T(8,128)} %get-tuple-element.19.dg_hbm, f32[512,896]{1,0:T(8,128)} %get-tuple-element.20.acc_hbm, f32[4,16,512]{2,1,0:T(8,128)} %get-tuple-element.21.pos_hbm, ...), custom_call_target="tpu_custom_call" | custom-call | tf_op jit(solution)/shard_map/moe_finish/pallas_call | solution.py:580

commit v4 on v3

--- a/solution.py
+++ b/solution.py
@@ -58,7 +58,7 @@
 
 def moe_kernel(ring, cap, x_hbm, u_hbm, ids_ref, gates_ref, w1_hbm, w3_hbm, w2_hbm,
                dg_out, acc_out, pos_out, g1_out, g3_out, g2_out, mid_hbm, fin_hbm, b1_hbm, b2_hbm, b3_hbm,
-               xa, xe, pos0, pos1, pos2, line0, line1, line2, sg0, sg1, sg2, sg3, dg0, dg1, dg2, dg3,
+               xa, xe, pos0, pos1, pos2, sent0, sent1, sent2, line0, line1, line2, sg0, sg1, sg2, sg3, dg0, dg1, dg2, dg3,
                gbuf, xv, dxb, bv, acc, w13, w2, dw13, dw2, dw1r, dw3r, dw2r,
                ld_s, ag_s, ag_r, far_s, far_r, p_s, p_r, w_s, w_r, sg_s, sg_r, dg_s, dg_r,
                s2_s, s2_r, s2_l, s3_s, s3_r, r1_s, r1_r, r1_l, r2_s, r2_r, r3_s, r3_r,
@@ -88,6 +88,7 @@
             for parity, groups in enumerate((even, odd)):
                 pl.when(lax.rem(c, 2) == parity)(functools.partial(body, groups))
     pos = (pos0, pos1, pos2)
+    sent = (sent0, sent1, sent2)
     line = (line0, line1, line2)
     strides = (ring * ring, ring, 1)
     me = lax.axis_index("ep")
@@ -142,13 +143,14 @@
         before = dot(chosen.astype(BF16), earlier)
         place = jnp.where((chosen > 0.5) & (before < cap), before, -1.0)
         pos[p][...] = place.reshape(ring, plane, tok)
+        sent[p][...] = place.astype(BF16).reshape(ring, plane, tok)
 
     pltpu.make_async_copy(pos0, pos_out, end_s.at[0]).start()
     pl.semaphore_wait(barrier, 3 * (ring - 1) + 1)
 
     for p in range(3):
         for d in range(1, ring):
-            send(pos[p].at[d], line[p].at[ring - d], p_s.at[p], p_r.at[p], peer(p, d))
+            send(sent[p].at[d], line[p].at[ring - d], p_s.at[p], p_r.at[p], peer(p, d))
 
     sides = sorted({1, ring - 1})
 
@@ -219,7 +221,7 @@
                 wait_bytes(at(gbuf, (array, slot), {axis: rest}, col), s2_s.at[array, slot, p])
 
             for d in range(ring):
-                hot = one_hot(pos[p][0] if d == 0 else line[p][d], c * ROWS)
+                hot = one_hot(pos[p][0] if d == 0 else line[p][d].astype(F32), c * ROWS)
                 for i in mine:
                     first = max(pieces[i][2].start, col.start)
                     end = min(pieces[i][2].start + pieces[i][2].size, col.start + col.size)
@@ -413,11 +415,17 @@
         def _():
             compute(k - 2)
 
+        @pl.when(k == chunks + 1)
+        def _():
+            small_start(2, dg0, dg1, dg_s, dg_r)
+            for i, (mine, theirs, _) in enumerate(grads):
+                send(mine(1 - core), theirs, dw_s.at[i], dw_r.at[i], other)
+
         @pl.when(k >= 3)
         def _():
             back_two(k - 3)
 
-        @pl.when(k >= 4)
+        @pl.when((k >= 4) & (k <= chunks))
         def _():
             back_three(k - 4)
 
@@ -429,25 +437,23 @@
 
     lax.fori_loop(0, chunks + 2, tick, 0)
     last_one = chunks - 1
-    small_start(2, dg0, dg1, dg_s, dg_r)
-    for i, (mine, theirs, _) in enumerate(grads):
-        send(mine(1 - core), theirs, dw_s.at[i], dw_r.at[i], other)
+    small_wait(2, dg1, dg_r)
+    small_start(1, dg1, dg2, dg_s, dg_r)
     back_two(last_one)
+    back_three(last_one - 2)
     combine(last_one - 3)
     back_three(last_one - 1)
-    small_wait(2, dg1, dg_r)
-    small_start(1, dg1, dg2, dg_s, dg_r)
-    combine(last_one - 2)
-    back_three(last_one)
     small_wait(1, dg2, dg_r)
     small_start(0, dg2, dg3, dg_s, dg_r)
+    back_three(last_one)
     for i, (mine, theirs, out) in enumerate(grads):
         wait_bytes(theirs, dw_r.at[i])
         theirs[...] += mine(core)[...]
         pltpu.make_async_copy(theirs, out, out_s.at[i]).start()
+    combine(last_one - 2)
+    gate_grads()
     combine(last_one - 1)
     pltpu.make_async_copy(acc, acc_out, end_s.at[1]).start()
-    gate_grads()
 
     for i in range(len(pieces)):
         for d in sides:
@@ -556,7 +562,7 @@
             out_specs=[local] + [hbm] * 10,
             scratch_shapes=[
                 vmem((2, ring, tok, hidden), BF16), vmem((ring, tok, 128), BF16),
-                *[vmem(table, F32)] * 6,
+                *[vmem(table, F32)] * 3, *[vmem(table, BF16)] * 6,
                 *[vmem(small, F32)] * 8,
                 vmem((2, 2, *cube), BF16), vmem((2, *cube), BF16), vmem((2, *cube), BF16), vmem(cube, BF16),
                 vmem((tok, hidden), F32),

time: 275 us -> 274 us (level)
  no operation moved by 1% of the time
where the time goes in v4:
time: 274 us
  Pallas kernels  273 us (100%)
    pallas_call x1, Pallas kernels, per_device(): pl.pallas_call(functools.partial(moe_kernel, ring, cap), out_shape=[sds((...  268 us

profile of v4, /device:TPU:0, one launch (start us, length us, event | category | flops | bytes accessed | tf_op | source)
XLA Modules:
  0.0 273.6 jit_solution(16248353290622277504)
XLA Ops:
  0.6 267.9 %moe_backward.1 = (f32[8,512]{1,0:T(8,128)}, f32[512,896]{1,0:T(8,128)}, f32[4,16,512]{2,1,0:T(8,128)}, f32[448,640]{1,0:T(8,128)}, f32[448,640]{1,0:T(8,128)}, ...) custom-call(bf16[512,896]{1,0:T(8,128)(2,1)} %x_hbm.1, ...), custom_call_target="tpu_custom_call" | custom-call | tf_op jit(solution)/shard_map/moe_backward/pallas_call | solution.py:553
  268.5 4.9 %moe_finish.1 = (bf16[512,896]{1,0:T(8,128)(2,1)}, f32[8,512]{1,0:T(8,128)}, f32[448,640]{1,0:T(8,128)}, f32[448,640]{1,0:T(8,128)}, f32[448,640]{1,0:T(8,128)}) custom-call(f32[8,512]{1,0:T(8,128)} %get-tuple-element.19.dg_hbm, f32[512,896]{1,0:T(8,128)} %get-tuple-element.20.acc_hbm, f32[4,16,512]{2,1,0:T(8,128)} %get-tuple-element.21.pos_hbm, ...), custom_call_target="tpu_custom_call" | custom-call | tf_op jit(solution)/shard_map/moe_finish/pallas_call | solution.py:586
